TPU v7x, 128 devices: a whole 4x4x4 slice. The times are simulated.
128 devices in a mesh: cand: 8 (over z, y_hi), ground: 16 (over x, y_lo, core).
Axes of the slice: x: 4, y: 4 (y_hi: 2, y_lo: 2; y = y_hi * 2 + y_lo), z: 4, core: 2. Of those that a mesh axis runs over, the one named last changes fastest.
Arguments:
- ground_rows: bfloat16 [131072, 1024], P('ground'), may hold values from -6 to 6
- best: float32 [131072], P('ground'), may hold values from -1.9 to 1.4
- cand_index: int32 [8192], P('cand'), may hold values from 0 to 131071
- chosen_index: int32 [64], replicated, may hold values from 0 to 131071
Outputs:
- gains: float32 [8192], P(('cand', 'ground'))
- new_best: float32 [131072], P('ground')
All inputs are finite; a program needn't handle non-finite values.
Results may differ from a plain program's by a relative error of at most 0.0003.
Values may be sent and summed in bfloat16 or wider, within the bound.
No kernel may reach another device: no remote copies, remote signals or barrier semaphores. Data moves between devices by JAX's collectives and lax.ppermute only.
A program may use at most 64 MiB of HBM per device.

v0:
```python
import jax
import jax.numpy as jnp
from jax import lax
from jax.experimental import pallas as pl
from jax.experimental.pallas import tpu as pltpu
from jax.sharding import PartitionSpec as P


CAP = 96
CAP_CHOSEN = 16
SLOTS = CAP + CAP_CHOSEN
LANES = 128
TILE = 8

F32 = jnp.float32
BF16 = jnp.bfloat16
I32 = jnp.int32


def iota(shape, dim):
    return lax.broadcasted_iota(I32, shape, dim)


def pick_kernel(turn_ref, cand_ref, chosen_ref, slab_ref, block_ref, rank_ref, counts_ref,
                pad_ref, list_ref, slots_ref, stage_ref, sem, list_sem):
    count = slab_ref.shape[0]
    shift = count.bit_length() - 1
    me = lax.axis_index("ground")
    turn = turn_ref[0]
    rows = cand_ref.shape[0]
    lane = iota((LANES, LANES), 1)
    line = iota((LANES, LANES), 0)
    upper = jnp.where(line <= lane, 1.0, 0.0).astype(BF16)

    pad_ref[...] = jnp.full(pad_ref.shape, -1, I32)
    pad_ref[0:1, 0 : chosen_ref.shape[1]] = chosen_ref[...]
    index = jnp.concatenate([cand_ref[...], pad_ref[...]], axis=0)
    mine = lax.shift_right_arithmetic(index, shift) == me
    upto = jnp.dot(jnp.where(mine, 1.0, 0.0).astype(BF16), upper, preferred_element_type=F32)
    ends = jnp.broadcast_to(upto[:, LANES - 1 : LANES], upto.shape)
    before = jnp.zeros((1, LANES), F32)
    lines = []
    for j in range(rows):
        lines.append(before)
        before = before + ends[j : j + 1, :]
    ahead = jnp.concatenate(lines + [jnp.zeros((8, LANES), F32)], axis=0)
    slot = (upto - 1.0 + ahead).astype(I32)
    top = iota(index.shape, 0) < rows
    slot = slot - turn * jnp.where(top, CAP, CAP_CHOSEN)
    inside = mine & (slot >= 0) & (slot < jnp.where(top, CAP, CAP_CHOSEN))
    slot = jnp.where(inside, jnp.where(top, slot, slot + CAP), -1)
    packed = jnp.where(inside, index - me * count, 0)
    slot_t = slot.T
    packed_t = packed.T
    found = jnp.zeros((LANES, LANES), I32)
    for j in range(rows + 1):
        found += jnp.where(slot_t[:, j : j + 1] == lane, packed_t[:, j : j + 1], 0)
    row = jnp.sum(found.astype(F32), axis=0, keepdims=True)
    row = jnp.broadcast_to(row, (8, LANES))
    list_ref[...] = row.astype(I32)
    copy = pltpu.make_async_copy(list_ref, slots_ref, list_sem)
    copy.start()
    copy.wait()
    for p in range(SLOTS):
        tile = lax.shift_right_logical(slots_ref[0, p], 3)
        pltpu.make_async_copy(slab_ref.at[pl.ds(pl.multiple_of(tile * TILE, TILE), TILE), :],
                              stage_ref.at[pl.ds(p * TILE, TILE), :], sem).start()

    lower = jnp.where(line >= lane, 1.0, 0.0).astype(BF16)
    index_t = index.T

    def ranked(col, carry):
        hot = lax.shift_right_arithmetic(col, shift) == lane
        upto = jnp.dot(lower, jnp.where(hot, 1.0, 0.0).astype(BF16), preferred_element_type=F32)
        rank = jnp.sum(jnp.where(hot, upto - 1.0 + carry, 0.0), axis=1, keepdims=True)
        return rank, carry + upto[LANES - 1 : LANES, :]

    counts = jnp.zeros((1, LANES), F32)
    ranks = []
    for j in range(rows):
        rank, counts = ranked(index_t[:, j : j + 1], counts)
        ranks.append(rank)
    rank_ref[...] = jnp.concatenate(ranks, axis=1).T.astype(I32)
    _, ccounts = ranked(index_t[:, rows : rows + 1], jnp.zeros((1, LANES), F32))
    turns = jnp.maximum(
        (jnp.max(counts, axis=1, keepdims=True).astype(I32) + CAP - 1) // CAP,
        (jnp.max(ccounts, axis=1, keepdims=True).astype(I32) + CAP_CHOSEN - 1) // CAP_CHOSEN,
    )
    counts_ref[0:1, :] = counts.astype(I32)
    counts_ref[1:2, :] = ccounts.astype(I32)
    counts_ref[2:3, :] = jnp.broadcast_to(turns, (1, LANES))

    inner = row.T[:, 0:1].astype(I32) & (TILE - 1)
    want = inner[:SLOTS] + TILE * iota((SLOTS, 1), 0)
    one = jnp.where(iota((SLOTS, SLOTS * TILE), 1) == want, 1.0, 0.0).astype(BF16)
    pltpu.make_async_copy(slab_ref.at[pl.ds(0, SLOTS * TILE), :], stage_ref, sem).wait()
    block_ref[...] = jnp.dot(one, stage_ref[...], preferred_element_type=F32).astype(BF16)


def pick(turn, cand, chosen, slab):
    width = slab.shape[1]
    return pl.pallas_call(
        pick_kernel,
        in_specs=[pl.BlockSpec(memory_space=pltpu.SMEM), pl.BlockSpec(memory_space=pltpu.VMEM),
                  pl.BlockSpec(memory_space=pltpu.VMEM), pl.BlockSpec(memory_space=pl.ANY)],
        out_specs=[pl.BlockSpec(memory_space=pltpu.VMEM)] * 3,
        out_shape=[pltpu.VMEM((SLOTS, width), BF16), pltpu.VMEM(cand.shape, I32), pltpu.VMEM((8, LANES), I32)],
        scratch_shapes=[pltpu.VMEM((8, LANES), I32), pltpu.VMEM((8, LANES), I32),
                        pltpu.SMEM((8, LANES), I32), pltpu.VMEM((SLOTS * TILE, width), BF16),
                        pltpu.SemaphoreType.DMA, pltpu.SemaphoreType.DMA],
        name="pick",
    )(turn, cand, chosen, slab)


def gain_kernel(turn_ref, counts_ref, cand_ref, rank_ref, before_ref, best_ref, slab_ref, *rest,
                peers, earlier, main, last, scale):
    blocks = rest[:peers]
    if last:
        out_ref, level_ref, dense_ref, acc_ref, at_ref, tall_ref, sems = rest[peers:]
    else:
        out_ref, dense_ref, acc_ref, at_ref, tall_ref, sems = rest[peers:]
        level_ref = None
    chunks, chunk, _ = tall_ref.shape
    count = slab_ref.shape[0]
    shift = count.bit_length() - 1
    total = cand_ref.shape[0] * cand_ref.shape[1]
    head = dense_ref.shape[0] - 2 * SLOTS - (total if last else main)
    turn = turn_ref[0]
    for i in range(chunks):
        pltpu.make_async_copy(slab_ref.at[pl.ds(i * chunk, chunk), :], tall_ref.at[i], sems.at[i]).start()

    sources = arrivals()[:peers]
    start = jnp.int32(0)
    done = jnp.int32(0)
    starts, heres = [], []
    for a in range(peers):
        if a == earlier:
            done = jnp.minimum(start, turn_ref[1])
        here = jnp.clip(counts_ref[0, sources[a]] - turn * CAP, 0, CAP)
        starts.append(start)
        heres.append(here)
        start = start + here
    stop = start if last else jnp.minimum(start, main)

    dense_ref[...] = jnp.zeros_like(dense_ref)
    acc_ref[...] = jnp.zeros_like(acc_ref)
    q = iota((1, 2 * SLOTS), 1)
    for a in range(0, peers, 2):

        @pl.when((starts[a] < stop) & (starts[a + 1] + heres[a + 1] > done))
        def _():
            row = jnp.where(q < SLOTS, q + starts[a], q - SLOTS + starts[a + 1])
            ends = jnp.where(q < SLOTS, starts[a] + heres[a], starts[a + 1] + heres[a + 1])
            good = (row < ends) & (row >= done) & (row < stop)
            target = jnp.where(good, row - done, -1)
            base = pl.multiple_of(jnp.maximum(starts[a] - done, 0) // 16 * 16, 16)
            one = jnp.where(iota((2 * SLOTS, 1), 0) + base == target, 1.0, 0.0).astype(BF16)
            pair = jnp.concatenate([blocks[a][...], blocks[a + 1][...]], axis=0)
            rows = jnp.dot(one, pair, preferred_element_type=F32)
            window = pl.ds(pl.multiple_of(base + head, 16), 2 * SLOTS)
            dense_ref[window, :] = (dense_ref[window, :].astype(F32) + rows).astype(BF16)

    there = jnp.int32(0)
    if last:
        q = iota((1, peers * CAP_CHOSEN), 1)
        target = jnp.full((1, peers * CAP_CHOSEN), -1, I32)
        for a in range(peers):
            here = jnp.clip(counts_ref[1, sources[a]] - turn * CAP_CHOSEN, 0, CAP_CHOSEN)
            slot = q - a * CAP_CHOSEN
            target = jnp.where((slot >= 0) & (slot < here), slot + there, target)
            there = there + here
        one = jnp.where(iota((head, 1), 0) == target, 1.0, 0.0).astype(BF16)
        rows = jnp.concatenate([block[CAP:SLOTS, :] for block in blocks], axis=0)
        dense_ref[0:head, :] = jnp.dot(one, rows, preferred_element_type=F32).astype(BF16)

    sub = 256
    per = chunk // LANES
    low = jnp.where(iota((max(head, 8), 1), 0) < there, 0.0, -jnp.inf)

    def add_up(i, first, size, with_head, tiles):
        lines = pl.ds(pl.multiple_of(i * per, per), per)
        level = best_ref[lines, :]
        scaled = level * (1.0 / scale)
        for u in tiles:
            sims = lax.dot_general(dense_ref[pl.ds(first, size), :], tall_ref[i, pl.ds(u * sub, sub), :],
                                   (((1,), (1,)), ((), ())), preferred_element_type=F32)
            skip = head if with_head else 0
            part = acc_ref[pl.ds(first + skip, size - skip), :]
            for j in range(sub // LANES):
                k = u * (sub // LANES) + j
                cols = sims[:, j * LANES : (j + 1) * LANES]
                part += jnp.maximum(cols[skip:] - scaled[k : k + 1, :], 0.0)
                if with_head:
                    top = jnp.max(cols[:skip] + low, axis=0, keepdims=True) * scale
                    level_ref[pl.ds(i * per + k, 1), :] = jnp.maximum(level[k : k + 1, :], top)
            acc_ref[pl.ds(first + skip, size - skip), :] = part

    def main_step(i, carry):
        pltpu.make_async_copy(slab_ref.at[pl.ds(0, chunk), :], tall_ref.at[i], sems.at[i]).wait()
        add_up(i, 0, head + main, last, range(chunk // sub))
        return carry

    lax.fori_loop(0, chunks, main_step, 0)

    slab = lax.shift_right_arithmetic(cand_ref[...], shift)
    slot = rank_ref[...] - turn * CAP
    place = jnp.full(slot.shape, -1, I32)
    for a in range(peers):
        place = jnp.where(slab == sources[a], slot + starts[a] - done, place)
    good = (slot >= 0) & (slot < CAP) & (place >= 0) & (place < stop - done)
    place = jnp.where(good, place, -1)

    def hand_out(ref, first, size):
        sums = jnp.sum(acc_ref[pl.ds(head + first, size), :], axis=1, keepdims=True) * scale
        at = iota((size, LANES), 0) + first
        for j in range(slot.shape[0]):
            mine = jnp.where(at == place[j : j + 1, :], sums, 0.0)
            out_ref[j : j + 1, :] = ref[j : j + 1, :] + jnp.sum(mine, axis=0, keepdims=True)

    hand_out(before_ref, 0, main)
    if last and total > main:

        @pl.when(stop - done > main)
        def _():
            def rest_step(k, carry):
                lines = sub // LANES
                edges = best_ref[pl.ds(k * lines, lines), :] * (1.0 / scale)
                i, u = k // (chunk // sub), k % (chunk // sub)
                tall = tall_ref[i, pl.ds(pl.multiple_of(u * sub, sub), sub), :]
                sims = lax.dot_general(dense_ref[pl.ds(head + main, total - main), :], tall,
                                       (((1,), (1,)), ((), ())), preferred_element_type=F32)
                for j in range(lines):
                    cols = sims[:, j * LANES : (j + 1) * LANES]
                    acc_ref[pl.ds(head + main, total - main), :] += jnp.maximum(cols - edges[j : j + 1, :], 0.0)
                return carry

            lax.fori_loop(0, chunks * (chunk // sub), rest_step, 0)
            hand_out(out_ref, main, total - main)


def gain(turn, counts, cand, rank, before, best, slab, blocks, earlier, main, chosen, scale):
    count, width = slab.shape
    total = cand.shape[0] * cand.shape[1]
    peers = len(blocks)
    last = chosen > 0
    chunk = min(2048, count)
    body = lambda *refs: gain_kernel(*refs, peers=peers, earlier=earlier, main=main, last=last, scale=scale)
    vmem = pl.BlockSpec(memory_space=pltpu.VMEM)
    outs = [jax.ShapeDtypeStruct(cand.shape, F32)] + [jax.ShapeDtypeStruct(best.shape, F32)] * last
    rows = chosen + (total if last else main)
    made = pl.pallas_call(
        body,
        in_specs=[pl.BlockSpec(memory_space=pltpu.SMEM)] * 2 + [vmem] * 4
        + [pl.BlockSpec(memory_space=pl.ANY)] + [vmem] * peers,
        out_specs=[vmem] * len(outs),
        out_shape=outs,
        scratch_shapes=[pltpu.VMEM((rows + 2 * SLOTS, width), BF16),
                        pltpu.VMEM((rows, LANES), F32),
                        pltpu.SMEM((8,), I32),
                        pltpu.VMEM((count // chunk, chunk, width), BF16),
                        pltpu.SemaphoreType.DMA((count // chunk,))],
        compiler_params=pltpu.CompilerParams(vmem_limit_bytes=40 * 2**20),
        cost_estimate=pl.CostEstimate(flops=2 * count * width * (main + chosen), transcendentals=0,
                                      bytes_accessed=2 * count * width),
        name="gain_last" if last else "gain",
    )(turn, counts, cand, rank, before, best, slab, *blocks)
    return made if last else made[0]


def device(x, y, c):
    return (x % 4) * 4 + y * 2 + c


def moved(array, dx, dy, dc):
    pairs = [(device(x, y, c), device(x + (dx if c == 0 else -dx), y ^ dy, c ^ dc))
             for x in range(4) for y in range(2) for c in range(2)]
    return lax.ppermute(array, "ground", pairs)


def arrivals():
    me = lax.axis_index("ground")
    x, y, c = me // 4, me // 2 % 2, me % 2
    sign = 1 - 2 * c
    near = [(0, y), (0, 1 - y), (-sign, y), (sign, y)]
    far = [(2, y), (-sign, 1 - y), (sign, 1 - y), (2, 1 - y)]
    here = lambda places: [(x + dx + 4) % 4 * 4 + yy * 2 + c for dx, yy in places]
    there = lambda places: [(x - dx + 4) % 4 * 4 + yy * 2 + 1 - c for dx, yy in places]
    return here(near) + there(near) + here(far) + there(far)


def near_blocks(own):
    ahead = moved(own, 1, 0, 0)
    behind = moved(own, -1, 0, 0)
    flip = moved(own, 0, 1, 0)
    return both_cores([own, flip, ahead, behind])


def far_blocks(near):
    own, _, ahead, _ = near[:4]
    across = moved(ahead, 1, 0, 0)
    flip_ahead = moved(own, 1, 1, 0)
    flip_behind = moved(own, -1, 1, 0)
    flip_across = moved(ahead, 1, 1, 0)
    return [across, flip_ahead, flip_behind, flip_across]


def both_cores(mine):
    return mine + [moved(block, 0, 0, 1) for block in mine]


def body(ground_rows, best, cand_index, chosen_index):
    count, width = ground_rows.shape
    scale = width ** (-0.5)
    peers = lax.axis_size("ground")
    whole = count * peers
    cand = cand_index.reshape(-1, LANES)
    chosen = chosen_index.reshape(1, -1)
    level = best.reshape(-1, LANES)
    total = cand_index.shape[0]
    first_rows = total * 13 // 32

    def finish(turn, limit, counts, rank, gains, level, blocks):
        state = jnp.stack([turn, limit]).astype(I32)
        return gain(state, counts, cand, rank, gains, level, ground_rows, blocks, peers // 2,
                    total - first_rows, chosen.shape[1], scale)

    block, rank, counts = pick(jnp.zeros((1,), I32), cand, chosen, ground_rows)
    turns = counts[2, 0]
    near = near_blocks(block)
    far = far_blocks(near)
    gains = gain(jnp.zeros((2,), I32), counts, cand, rank, jnp.zeros(cand.shape, F32), level, ground_rows, near,
                 0, first_rows, 0, scale)
    gains, far = lax.optimization_barrier((gains, far))
    far = both_cores(far)
    gains, new = finish(jnp.int32(0), jnp.int32(first_rows), counts, rank, gains, level, near + far)

    def more(state):
        return state[0] < turns

    def again(state):
        turn, gains, new = state
        block, rank, counts = pick(turn.reshape(1), cand, chosen, ground_rows)
        near = near_blocks(block)
        added, raised = finish(turn, jnp.int32(0), counts, rank, gains, level, near + both_cores(far_blocks(near)))
        return turn + 1, added, jnp.maximum(new, raised)

    _, gains, new = lax.while_loop(more, again, (jnp.int32(1), gains, new))
    blocks = gains.reshape(peers, -1) / whole
    arrived = lax.all_to_all(blocks, "ground", 0, 0, tiled=True)
    return arrived.sum(axis=0), new.reshape(-1)


def solution(mesh):
    in_specs = (P("ground", None), P("ground"), P("cand"), P())
    out_specs = (P(("cand", "ground")), P("ground"))
    return jax.shard_map(body, mesh=mesh, in_specs=in_specs, out_specs=out_specs, check_vma=False)
```

profile of v0, /device:TPU:1, one launch (start us, length us, event | category | flops | bytes accessed | tf_op | source)
XLA Modules:
  0.0 67.7 jit_solution(9500779149743172571)
XLA Ops:
  0.6 6.0 %pick.2 = (bf16[112,1024]{1,0:T(8,128)(2,1)S(1)}, s32[8,128]{1,0:T(8,128)S(1)}, s32[8,128]{1,0:T(8,128)S(1)}) custom-call(s32[1]{0:T(128)} %constant.4.clone.1.turn_ref, s32[8,128]{1,0:T(8,128)} %bitcast.9, s32[1,64]{1,0:T(1,128)} %bitcast.13, bf16[8192,1024]{1,0:T(8,128)(2,1)} %refs_6_.3), custom_call_target="tpu_custom_call" | custom-call | tf_op jit(solution)/shard_map/pick/pallas_call | solution.py:102
  6.7 2.7 %collective-permute-start.17 = (bf16[112,1024]{1,0:T(8,128)(2,1)S(1)}, bf16[112,1024]{1,0:T(8,128)(2,1)S(1)}, u32[]{:S(2)}, u32[]{:S(2)}) collective-permute-start(bf16[112,1024]{1,0:T(8,128)(2,1)S(1)} %get-tuple-element.63.refs_7_), channel_id=1, source_target_pairs={{0,12},{1,5},{2,14},{3,7},{4,0},{5,9},{6,2},{7,11},{8,4},{9,13},{1... | collective-permute-start | bytes 688136 | tf_op jit(solution)/shard_map/ppermute | solution.py:277
  9.4 1.2 %collective-permute-start.16 = (bf16[112,1024]{1,0:T(8,128)(2,1)S(1)}, bf16[112,1024]{1,0:T(8,128)(2,1)S(1)}, u32[]{:S(2)}, u32[]{:S(2)}) collective-permute-start(bf16[112,1024]{1,0:T(8,128)(2,1)S(1)} %get-tuple-element.63.refs_7_), channel_id=1, source_target_pairs={{0,4},{1,13},{2,6},{3,15},{4,8},{5,1},{6,10},{7,3},{8,12},{9,5},{1... | collective-permute-start | bytes 688136 | tf_op jit(solution)/shard_map/ppermute | solution.py:277
  10.6 1.5 %collective-permute-start.15 = (bf16[112,1024]{1,0:T(8,128)(2,1)S(1)}, bf16[112,1024]{1,0:T(8,128)(2,1)S(1)}, u32[]{:S(2)}, u32[]{:S(2)}) collective-permute-start(bf16[112,1024]{1,0:T(8,128)(2,1)S(1)} %get-tuple-element.63.refs_7_), channel_id=1, source_target_pairs={{0,2},{1,3},{2,0},{3,1},{4,6},{5,7},{6,4},{7,5},{8,10},{9,11},{10,... | collective-permute-start | bytes 688136 | tf_op jit(solution)/shard_map/ppermute | solution.py:277
  12.1 0.8 %collective-permute-start.18 = (bf16[112,1024]{1,0:T(8,128)(2,1)S(1)}, bf16[112,1024]{1,0:T(8,128)(2,1)S(1)}, u32[]{:S(2)}, u32[]{:S(2)}) collective-permute-start(bf16[112,1024]{1,0:T(8,128)(2,1)S(1)} %get-tuple-element.63.refs_7_), channel_id=1, source_target_pairs={{0,1},{1,0},{2,3},{3,2},{4,5},{5,4},{6,7},{7,6},{8,9},{9,8},{10,11... | collective-permute-start | bytes 688136 | tf_op jit(solution)/shard_map/ppermute | solution.py:277
  12.9 1.1 %collective-permute-done.17.refs_10_ = bf16[112,1024]{1,0:T(8,128)(2,1)S(1)} collective-permute-done((bf16[112,1024]{1,0:T(8,128)(2,1)S(1)}, bf16[112,1024]{1,0:T(8,128)(2,1)S(1)}, u32[]{:S(2)}, u32[]{:S(2)}) %collective-permute-start.17) | collective-permute-done | bytes 229408 | tf_op jit(solution)/shard_map/ppermute | solution.py:277
  13.9 2.5 %collective-permute-start.21 = (bf16[112,1024]{1,0:T(8,128)(2,1)S(1)}, bf16[112,1024]{1,0:T(8,128)(2,1)S(1)}, u32[]{:S(2)}, u32[]{:S(2)}) collective-permute-start(bf16[112,1024]{1,0:T(8,128)(2,1)S(1)} %collective-permute-done.17.refs_10_), channel_id=1, source_target_pairs={{0,1},{1,0},{2,3},{3,2},{4,5},{5,4},{6,7},{7,6},{8,9},{9,8},{10,11... | collective-permute-start | bytes 688136 | tf_op jit(solution)/shard_map/ppermute | solution.py:277
  16.4 2.2 %collective-permute-start.20 = (bf16[112,1024]{1,0:T(8,128)(2,1)S(1)}, bf16[112,1024]{1,0:T(8,128)(2,1)S(1)}, u32[]{:S(2)}, u32[]{:S(2)}) collective-permute-start(bf16[112,1024]{1,0:T(8,128)(2,1)S(1)} %collective-permute-done.16.refs_9_), channel_id=1, source_target_pairs={{0,1},{1,0},{2,3},{3,2},{4,5},{5,4},{6,7},{7,6},{8,9},{9,8},{10,11... | collective-permute-start | bytes 688136 | tf_op jit(solution)/shard_map/ppermute | solution.py:277
  18.6 0.9 %collective-permute-start.24 = (bf16[112,1024]{1,0:T(8,128)(2,1)S(1)}, bf16[112,1024]{1,0:T(8,128)(2,1)S(1)}, u32[]{:S(2)}, u32[]{:S(2)}) collective-permute-start(bf16[112,1024]{1,0:T(8,128)(2,1)S(1)} %get-tuple-element.63.refs_7_), channel_id=1, source_target_pairs={{0,14},{1,7},{2,12},{3,5},{4,2},{5,11},{6,0},{7,9},{8,6},{9,15},{1... | collective-permute-start | bytes 688136 | tf_op jit(solution)/shard_map/ppermute | solution.py:277
  19.6 2.6 %collective-permute-start.23 = (bf16[112,1024]{1,0:T(8,128)(2,1)S(1)}, bf16[112,1024]{1,0:T(8,128)(2,1)S(1)}, u32[]{:S(2)}, u32[]{:S(2)}) collective-permute-start(bf16[112,1024]{1,0:T(8,128)(2,1)S(1)} %get-tuple-element.63.refs_7_), channel_id=1, source_target_pairs={{0,6},{1,15},{2,4},{3,13},{4,10},{5,3},{6,8},{7,1},{8,14},{9,7},{1... | collective-permute-start | bytes 688136 | tf_op jit(solution)/shard_map/ppermute | solution.py:277
  22.2 1.7 %collective-permute-start.25 = (bf16[112,1024]{1,0:T(8,128)(2,1)S(1)}, bf16[112,1024]{1,0:T(8,128)(2,1)S(1)}, u32[]{:S(2)}, u32[]{:S(2)}) collective-permute-start(bf16[112,1024]{1,0:T(8,128)(2,1)S(1)} %collective-permute-done.16.refs_9_), channel_id=1, source_target_pairs={{0,6},{1,15},{2,4},{3,13},{4,10},{5,3},{6,8},{7,1},{8,14},{9,7},{1... | collective-permute-start | bytes 688136 | tf_op jit(solution)/shard_map/ppermute | solution.py:277
  24.0 11.0 %gain.1.refs_4_ = f32[8,128]{1,0:T(8,128)S(1)} custom-call(s32[2]{0:T(128)S(1)} %broadcast_1_refs_0_.2.refs_0_, s32[8,128]{1,0:T(8,128)S(1)} %get-tuple-element.61.refs_1_, s32[8,128]{1,0:T(8,128)S(1)} %bitcast.10, s32[8,128]{1,0:T(8,128)S(1)} %get-tuple-element.62.refs_3_, f32[8,128]{1,0:T(8,128)S(1)} %broadcast_in_dim.3.refs_4_, f32[64,128]{1,0:T(8,128)S(1)} %bitcast.15, ...), custom_call_target="tpu_custom_call" | custom-call | flops 6979321856 | bytes 16777216 | tf_op jit(solution)/shard_map/gain/pallas_call | solution.py:251
  35.1 2.6 %collective-permute-done.25.refs_18_ = bf16[112,1024]{1,0:T(8,128)(2,1)S(1)} collective-permute-done((bf16[112,1024]{1,0:T(8,128)(2,1)S(1)}, bf16[112,1024]{1,0:T(8,128)(2,1)S(1)}, u32[]{:S(2)}, u32[]{:S(2)}) %collective-permute-start.25) | collective-permute-done | bytes 229408 | tf_op jit(solution)/shard_map/ppermute | solution.py:277
  37.7 1.7 %collective-permute-done.22.refs_15_ = bf16[112,1024]{1,0:T(8,128)(2,1)S(1)} collective-permute-done((bf16[112,1024]{1,0:T(8,128)(2,1)S(1)}, bf16[112,1024]{1,0:T(8,128)(2,1)S(1)}, u32[]{:S(2)}, u32[]{:S(2)}) %collective-permute-start.22) | collective-permute-done | bytes 229408 | tf_op jit(solution)/shard_map/ppermute | solution.py:277
  39.4 0.5 collective-permute-start.27
  39.9 0.5 collective-permute-start.29
  40.4 0.5 slice.3
  40.9 0.3 collective-permute-done.27.refs_20_
  41.2 0.3 collective-permute-done.28.refs_21_
  41.5 0.5 collective-permute-done.29.refs_22_
  42.0 15.8 %gain_last.2 = (f32[8,128]{1,0:T(8,128)S(1)}, f32[64,128]{1,0:T(8,128)S(1)}) custom-call(s32[2]{0:T(128)S(1)} %iota_multiply_fusion.refs_0_, s32[8,128]{1,0:T(8,128)S(1)} %get-tuple-element.61.refs_1_, s32[8,128]{1,0:T(8,128)S(1)} %bitcast.11, s32[8,128]{1,0:T(8,128)S(1)} %get-tuple-element.62.refs_3_, f32[8,128]{1,0:T(8,128)S(1)} %gain.1.refs_4_, ...), custom_call_target="tpu_custom_call" | custom-call | flops 11274289152 | bytes 16777216 | tf_op jit(solution)/shard_map/gain_last/pallas_call | solution.py:251
  57.8 0.7 while.12
  58.6 8.6 %all_to_all.6 = f32[16,1,64]{2,1,0:T(1,128)S(1)} all-to-all(f32[16,1,64]{2,1,0:T(1,128)S(1)} %div.10), channel_id=1, replica_groups=mesh['cand'=8,'ground'=16] {'ground'}, dimensions={0} | all-to-all | bytes 8192 | tf_op jit(solution)/shard_map/all_to_all | solution.py:349
  67.2 0.5 reduce_sum.9
  (26 shorter events, 0.2 us)
Async XLA Ops:
  0.6 23.3 %copy-start.1 = (s32[1024]{0:T(1024)S(1)}, s32[1024]{0:T(1024)}, u32[]{:S(2)}) copy-start(s32[1024]{0:T(1024)} %param.8) | copy-start | bytes 12292
  0.6 23.3 %copy-start.3 = (f32[8192]{0:T(1024)S(1)}, f32[8192]{0:T(1024)}, u32[]{:S(2)}) copy-start(f32[8192]{0:T(1024)} %param.7) | copy-start | bytes 98308
  6.7 7.2 %collective-permute-start.17 = (bf16[112,1024]{1,0:T(8,128)(2,1)S(1)}, bf16[112,1024]{1,0:T(8,128)(2,1)S(1)}, u32[]{:S(2)}, u32[]{:S(2)}) collective-permute-start(bf16[112,1024]{1,0:T(8,128)(2,1)S(1)} %get-tuple-element.63.refs_7_), channel_id=1, source_target_pairs={{0,12},{1,5},{2,14},{3,7},{4,0},{5,9},{6,2},{7,11},{8,4},{9,13},{1... | collective-permute-start | bytes 688136 | tf_op jit(solution)/shard_map/ppermute | solution.py:277
  9.4 7.1 %collective-permute-start.16 = (bf16[112,1024]{1,0:T(8,128)(2,1)S(1)}, bf16[112,1024]{1,0:T(8,128)(2,1)S(1)}, u32[]{:S(2)}, u32[]{:S(2)}) collective-permute-start(bf16[112,1024]{1,0:T(8,128)(2,1)S(1)} %get-tuple-element.63.refs_7_), channel_id=1, source_target_pairs={{0,4},{1,13},{2,6},{3,15},{4,8},{5,1},{6,10},{7,3},{8,12},{9,5},{1... | collective-permute-start | bytes 688136 | tf_op jit(solution)/shard_map/ppermute | solution.py:277
  10.6 8.0 %collective-permute-start.15 = (bf16[112,1024]{1,0:T(8,128)(2,1)S(1)}, bf16[112,1024]{1,0:T(8,128)(2,1)S(1)}, u32[]{:S(2)}, u32[]{:S(2)}) collective-permute-start(bf16[112,1024]{1,0:T(8,128)(2,1)S(1)} %get-tuple-element.63.refs_7_), channel_id=1, source_target_pairs={{0,2},{1,3},{2,0},{3,1},{4,6},{5,7},{6,4},{7,5},{8,10},{9,11},{10,... | collective-permute-start | bytes 688136 | tf_op jit(solution)/shard_map/ppermute | solution.py:277
  12.1 7.5 %collective-permute-start.18 = (bf16[112,1024]{1,0:T(8,128)(2,1)S(1)}, bf16[112,1024]{1,0:T(8,128)(2,1)S(1)}, u32[]{:S(2)}, u32[]{:S(2)}) collective-permute-start(bf16[112,1024]{1,0:T(8,128)(2,1)S(1)} %get-tuple-element.63.refs_7_), channel_id=1, source_target_pairs={{0,1},{1,0},{2,3},{3,2},{4,5},{5,4},{6,7},{7,6},{8,9},{9,8},{10,11... | collective-permute-start | bytes 688136 | tf_op jit(solution)/shard_map/ppermute | solution.py:277
  13.9 8.3 %collective-permute-start.21 = (bf16[112,1024]{1,0:T(8,128)(2,1)S(1)}, bf16[112,1024]{1,0:T(8,128)(2,1)S(1)}, u32[]{:S(2)}, u32[]{:S(2)}) collective-permute-start(bf16[112,1024]{1,0:T(8,128)(2,1)S(1)} %collective-permute-done.17.refs_10_), channel_id=1, source_target_pairs={{0,1},{1,0},{2,3},{3,2},{4,5},{5,4},{6,7},{7,6},{8,9},{9,8},{10,11... | collective-permute-start | bytes 688136 | tf_op jit(solution)/shard_map/ppermute | solution.py:277
  16.4 7.5 %collective-permute-start.20 = (bf16[112,1024]{1,0:T(8,128)(2,1)S(1)}, bf16[112,1024]{1,0:T(8,128)(2,1)S(1)}, u32[]{:S(2)}, u32[]{:S(2)}) collective-permute-start(bf16[112,1024]{1,0:T(8,128)(2,1)S(1)} %collective-permute-done.16.refs_9_), channel_id=1, source_target_pairs={{0,1},{1,0},{2,3},{3,2},{4,5},{5,4},{6,7},{7,6},{8,9},{9,8},{10,11... | collective-permute-start | bytes 688136 | tf_op jit(solution)/shard_map/ppermute | solution.py:277
  18.6 5.3 %collective-permute-start.19 = (bf16[112,1024]{1,0:T(8,128)(2,1)S(1)}, bf16[112,1024]{1,0:T(8,128)(2,1)S(1)}, u32[]{:S(2)}, u32[]{:S(2)}) collective-permute-start(bf16[112,1024]{1,0:T(8,128)(2,1)S(1)} %collective-permute-done.15.refs_8_), channel_id=1, source_target_pairs={{0,1},{1,0},{2,3},{3,2},{4,5},{5,4},{6,7},{7,6},{8,9},{9,8},{10,11... | collective-permute-start | bytes 688136 | tf_op jit(solution)/shard_map/ppermute | solution.py:277
  18.6 16.4 %collective-permute-start.24 = (bf16[112,1024]{1,0:T(8,128)(2,1)S(1)}, bf16[112,1024]{1,0:T(8,128)(2,1)S(1)}, u32[]{:S(2)}, u32[]{:S(2)}) collective-permute-start(bf16[112,1024]{1,0:T(8,128)(2,1)S(1)} %get-tuple-element.63.refs_7_), channel_id=1, source_target_pairs={{0,14},{1,7},{2,12},{3,5},{4,2},{5,11},{6,0},{7,9},{8,6},{9,15},{1... | collective-permute-start | bytes 688136 | tf_op jit(solution)/shard_map/ppermute | solution.py:277
  19.6 15.5 %collective-permute-start.23 = (bf16[112,1024]{1,0:T(8,128)(2,1)S(1)}, bf16[112,1024]{1,0:T(8,128)(2,1)S(1)}, u32[]{:S(2)}, u32[]{:S(2)}) collective-permute-start(bf16[112,1024]{1,0:T(8,128)(2,1)S(1)} %get-tuple-element.63.refs_7_), channel_id=1, source_target_pairs={{0,6},{1,15},{2,4},{3,13},{4,10},{5,3},{6,8},{7,1},{8,14},{9,7},{1... | collective-permute-start | bytes 688136 | tf_op jit(solution)/shard_map/ppermute | solution.py:277
  22.2 15.4 %collective-permute-start.25 = (bf16[112,1024]{1,0:T(8,128)(2,1)S(1)}, bf16[112,1024]{1,0:T(8,128)(2,1)S(1)}, u32[]{:S(2)}, u32[]{:S(2)}) collective-permute-start(bf16[112,1024]{1,0:T(8,128)(2,1)S(1)} %collective-permute-done.16.refs_9_), channel_id=1, source_target_pairs={{0,6},{1,15},{2,4},{3,13},{4,10},{5,3},{6,8},{7,1},{8,14},{9,7},{1... | collective-permute-start | bytes 688136 | tf_op jit(solution)/shard_map/ppermute | solution.py:277
  23.9 15.5 %collective-permute-start.22 = (bf16[112,1024]{1,0:T(8,128)(2,1)S(1)}, bf16[112,1024]{1,0:T(8,128)(2,1)S(1)}, u32[]{:S(2)}, u32[]{:S(2)}) collective-permute-start(bf16[112,1024]{1,0:T(8,128)(2,1)S(1)} %collective-permute-done.16.refs_9_), channel_id=1, source_target_pairs={{0,4},{1,13},{2,6},{3,15},{4,8},{5,1},{6,10},{7,3},{8,12},{9,5},{1... | collective-permute-start | bytes 688136 | tf_op jit(solution)/shard_map/ppermute | solution.py:277
  39.4 1.5 %collective-permute-start.26 = (bf16[112,1024]{1,0:T(8,128)(2,1)S(1)}, bf16[112,1024]{1,0:T(8,128)(2,1)S(1)}, u32[]{:S(2)}, u32[]{:S(2)}) collective-permute-start(bf16[112,1024]{1,0:T(8,128)(2,1)S(1)} %collective-permute-done.22.refs_15_), channel_id=1, source_target_pairs={{0,1},{1,0},{2,3},{3,2},{4,5},{5,4},{6,7},{7,6},{8,9},{9,8},{10,11... | collective-permute-start | bytes 688136 | tf_op jit(solution)/shard_map/ppermute | solution.py:277
  39.4 1.8 %collective-permute-start.27 = (bf16[112,1024]{1,0:T(8,128)(2,1)S(1)}, bf16[112,1024]{1,0:T(8,128)(2,1)S(1)}, u32[]{:S(2)}, u32[]{:S(2)}) collective-permute-start(bf16[112,1024]{1,0:T(8,128)(2,1)S(1)} %collective-permute-done.23.refs_16_), channel_id=1, source_target_pairs={{0,1},{1,0},{2,3},{3,2},{4,5},{5,4},{6,7},{7,6},{8,9},{9,8},{10,11... | collective-permute-start | bytes 688136 | tf_op jit(solution)/shard_map/ppermute | solution.py:277
  39.9 1.6 %collective-permute-start.28 = (bf16[112,1024]{1,0:T(8,128)(2,1)S(1)}, bf16[112,1024]{1,0:T(8,128)(2,1)S(1)}, u32[]{:S(2)}, u32[]{:S(2)}) collective-permute-start(bf16[112,1024]{1,0:T(8,128)(2,1)S(1)} %collective-permute-done.24.refs_17_), channel_id=1, source_target_pairs={{0,1},{1,0},{2,3},{3,2},{4,5},{5,4},{6,7},{7,6},{8,9},{9,8},{10,11... | collective-permute-start | bytes 688136 | tf_op jit(solution)/shard_map/ppermute | solution.py:277
  39.9 2.1 %collective-permute-start.29 = (bf16[112,1024]{1,0:T(8,128)(2,1)S(1)}, bf16[112,1024]{1,0:T(8,128)(2,1)}, u32[]{:S(2)}, u32[]{:S(2)}) collective-permute-start(bf16[112,1024]{1,0:T(8,128)(2,1)S(1)} %collective-permute-done.25.refs_18_), channel_id=1, source_target_pairs={{0,1},{1,0},{2,3},{3,2},{4,5},{5,4},{6,7},{7,6},{8,9},{9,8},{10,11... | collective-permute-start | bytes 688136 | tf_op jit(solution)/shard_map/ppermute | solution.py:277
  40.9 16.9 %copy-start.2 = (s32[64]{0:T(128)S(1)}, s32[64]{0:T(128)}, u32[]{:S(2)}) copy-start(s32[64]{0:T(128)} %param.9) | copy-start | bytes 772
  58.5 9.2 %copy-start = (f32[64,128]{1,0:T(8,128)}, f32[64,128]{1,0:T(8,128)S(1)}, u32[]{:S(2)}) copy-start(f32[64,128]{1,0:T(8,128)S(1)} %get-tuple-element.72) | copy-start | bytes 98308
where the time goes:
time: 68.1 us; the launch traced here: 67.7 us
  Pallas kernels  32.9 us (48%)
  starting transfers between devices  17.2 us (25%)
  blocking collectives  8.59 us (13%)
  waiting for transfers between devices  6.49 us (10%)
  between operations  0.77 us (1%)
    pallas_call x2, Pallas kernels, gain(): pl.pallas_call(body, in_specs=[pl.BlockSpec(memory_space=pltpu.SMEM)] * 2...  26.8 us
    ppermute x15, starting transfers between devices, moved(): return lax.ppermute(array, 'ground', pairs)  17.2 us
    all_to_all x1, blocking collectives, body(): arrived = lax.all_to_all(blocks, 'ground', 0, 0, tiled=True)  8.59 us
    ppermute x15, waiting for transfers between devices, moved(): return lax.ppermute(array, 'ground', pairs)  6.49 us
    pallas_call x1, Pallas kernels, pick(): pl.pallas_call(pick_kernel, in_specs=[pl.BlockSpec(memory_space=pltpu.SME...  6.04 us
  transfers between devices with their start and end apart: 15, of which 6 were waited for; matrix products, arithmetic and copies ran while one was open for 1% of the time, Pallas kernels for 16%

commit v1 on v0

--- a/solution.py
+++ b/solution.py
@@ -108,27 +108,27 @@
         scratch_shapes=[pltpu.VMEM((8, LANES), I32), pltpu.VMEM((8, LANES), I32),
                         pltpu.SMEM((8, LANES), I32), pltpu.VMEM((SLOTS * TILE, width), BF16),
                         pltpu.SemaphoreType.DMA, pltpu.SemaphoreType.DMA],
+        compiler_params=pltpu.CompilerParams(vmem_limit_bytes=16 * 2**20),
         name="pick",
     )(turn, cand, chosen, slab)
 
 
 def gain_kernel(turn_ref, counts_ref, cand_ref, rank_ref, before_ref, best_ref, slab_ref, *rest,
                 peers, earlier, main, last, scale):
-    blocks = rest[:peers]
+    pairs = rest[: peers // 2]
+    rest = rest[peers // 2 :]
     if last:
-        out_ref, level_ref, dense_ref, acc_ref, at_ref, tall_ref, sems = rest[peers:]
+        out_ref, level_ref, dense_ref, acc_ref = rest
     else:
-        out_ref, dense_ref, acc_ref, at_ref, tall_ref, sems = rest[peers:]
+        out_ref, dense_ref, acc_ref = rest
         level_ref = None
-    chunks, chunk, _ = tall_ref.shape
-    count = slab_ref.shape[0]
+    count, _ = slab_ref.shape
+    chunk = min(2048, count)
+    chunks = count // chunk
     shift = count.bit_length() - 1
     total = cand_ref.shape[0] * cand_ref.shape[1]
     head = dense_ref.shape[0] - 2 * SLOTS - (total if last else main)
     turn = turn_ref[0]
-    for i in range(chunks):
-        pltpu.make_async_copy(slab_ref.at[pl.ds(i * chunk, chunk), :], tall_ref.at[i], sems.at[i]).start()
-
     sources = arrivals()[:peers]
     start = jnp.int32(0)
     done = jnp.int32(0)
@@ -155,8 +155,7 @@
             target = jnp.where(good, row - done, -1)
             base = pl.multiple_of(jnp.maximum(starts[a] - done, 0) // 16 * 16, 16)
             one = jnp.where(iota((2 * SLOTS, 1), 0) + base == target, 1.0, 0.0).astype(BF16)
-            pair = jnp.concatenate([blocks[a][...], blocks[a + 1][...]], axis=0)
-            rows = jnp.dot(one, pair, preferred_element_type=F32)
+            rows = jnp.dot(one, pairs[a // 2][...], preferred_element_type=F32)
             window = pl.ds(pl.multiple_of(base + head, 16), 2 * SLOTS)
             dense_ref[window, :] = (dense_ref[window, :].astype(F32) + rows).astype(BF16)
 
@@ -170,7 +169,7 @@
             target = jnp.where((slot >= 0) & (slot < here), slot + there, target)
             there = there + here
         one = jnp.where(iota((head, 1), 0) == target, 1.0, 0.0).astype(BF16)
-        rows = jnp.concatenate([block[CAP:SLOTS, :] for block in blocks], axis=0)
+        rows = jnp.concatenate([pairs[a // 2][a % 2 * SLOTS + CAP : a % 2 * SLOTS + SLOTS, :] for a in range(peers)], axis=0)
         dense_ref[0:head, :] = jnp.dot(one, rows, preferred_element_type=F32).astype(BF16)
 
     sub = 256
@@ -182,7 +181,7 @@
         level = best_ref[lines, :]
         scaled = level * (1.0 / scale)
         for u in tiles:
-            sims = lax.dot_general(dense_ref[pl.ds(first, size), :], tall_ref[i, pl.ds(u * sub, sub), :],
+            sims = lax.dot_general(dense_ref[pl.ds(first, size), :], slab_ref[pl.ds(pl.multiple_of(i * chunk + u * sub, sub), sub), :],
                                    (((1,), (1,)), ((), ())), preferred_element_type=F32)
             skip = head if with_head else 0
             part = acc_ref[pl.ds(first + skip, size - skip), :]
@@ -196,7 +195,6 @@
             acc_ref[pl.ds(first + skip, size - skip), :] = part
 
     def main_step(i, carry):
-        pltpu.make_async_copy(slab_ref.at[pl.ds(0, chunk), :], tall_ref.at[i], sems.at[i]).wait()
         add_up(i, 0, head + main, last, range(chunk // sub))
         return carry
 
@@ -225,8 +223,7 @@
             def rest_step(k, carry):
                 lines = sub // LANES
                 edges = best_ref[pl.ds(k * lines, lines), :] * (1.0 / scale)
-                i, u = k // (chunk // sub), k % (chunk // sub)
-                tall = tall_ref[i, pl.ds(pl.multiple_of(u * sub, sub), sub), :]
+                tall = slab_ref[pl.ds(pl.multiple_of(k * sub, sub), sub), :]
                 sims = lax.dot_general(dense_ref[pl.ds(head + main, total - main), :], tall,
                                        (((1,), (1,)), ((), ())), preferred_element_type=F32)
                 for j in range(lines):
@@ -238,12 +235,11 @@
             hand_out(out_ref, main, total - main)
 
 
-def gain(turn, counts, cand, rank, before, best, slab, blocks, earlier, main, chosen, scale):
+def gain(turn, counts, cand, rank, before, best, slab, pairs, earlier, main, chosen, scale):
     count, width = slab.shape
     total = cand.shape[0] * cand.shape[1]
-    peers = len(blocks)
+    peers = 2 * len(pairs)
     last = chosen > 0
-    chunk = min(2048, count)
     body = lambda *refs: gain_kernel(*refs, peers=peers, earlier=earlier, main=main, last=last, scale=scale)
     vmem = pl.BlockSpec(memory_space=pltpu.VMEM)
     outs = [jax.ShapeDtypeStruct(cand.shape, F32)] + [jax.ShapeDtypeStruct(best.shape, F32)] * last
@@ -251,19 +247,16 @@
     made = pl.pallas_call(
         body,
         in_specs=[pl.BlockSpec(memory_space=pltpu.SMEM)] * 2 + [vmem] * 4
-        + [pl.BlockSpec(memory_space=pl.ANY)] + [vmem] * peers,
+        + [vmem] + [vmem] * len(pairs),
         out_specs=[vmem] * len(outs),
         out_shape=outs,
         scratch_shapes=[pltpu.VMEM((rows + 2 * SLOTS, width), BF16),
-                        pltpu.VMEM((rows, LANES), F32),
-                        pltpu.SMEM((8,), I32),
-                        pltpu.VMEM((count // chunk, chunk, width), BF16),
-                        pltpu.SemaphoreType.DMA((count // chunk,))],
-        compiler_params=pltpu.CompilerParams(vmem_limit_bytes=40 * 2**20),
+                        pltpu.VMEM((rows, LANES), F32)],
+        compiler_params=pltpu.CompilerParams(vmem_limit_bytes=24 * 2**20),
         cost_estimate=pl.CostEstimate(flops=2 * count * width * (main + chosen), transcendentals=0,
                                       bytes_accessed=2 * count * width),
         name="gain_last" if last else "gain",
-    )(turn, counts, cand, rank, before, best, slab, *blocks)
+    )(turn, counts, cand, rank, before, best, slab, *pairs)
     return made if last else made[0]
 
 
@@ -281,31 +274,41 @@
     me = lax.axis_index("ground")
     x, y, c = me // 4, me // 2 % 2, me % 2
     sign = 1 - 2 * c
-    near = [(0, y), (0, 1 - y), (-sign, y), (sign, y)]
-    far = [(2, y), (-sign, 1 - y), (sign, 1 - y), (2, 1 - y)]
+    near = [(0, y), (-sign, y), (sign, y), (0, 1 - y)]
+    far = [(2, y), (sign, 1 - y), (-sign, 1 - y), (2, 1 - y)]
     here = lambda places: [(x + dx + 4) % 4 * 4 + yy * 2 + c for dx, yy in places]
     there = lambda places: [(x - dx + 4) % 4 * 4 + yy * 2 + 1 - c for dx, yy in places]
     return here(near) + there(near) + here(far) + there(far)
 
 
-def near_blocks(own):
+def join_kernel(own_ref, ahead_ref, behind_ref, flip_ref, first_ref, second_ref):
+    first_ref[0:SLOTS, :] = own_ref[...]
+    first_ref[SLOTS : 2 * SLOTS, :] = ahead_ref[...]
+    second_ref[0:SLOTS, :] = behind_ref[...]
+    second_ref[SLOTS : 2 * SLOTS, :] = flip_ref[...]
+
+
+def join(*blocks):
+    vmem = pl.BlockSpec(memory_space=pltpu.VMEM)
+    pair = pltpu.VMEM((2 * SLOTS, blocks[0].shape[1]), BF16)
+    return pl.pallas_call(join_kernel, in_specs=[vmem] * 4, out_specs=[vmem] * 2, out_shape=[pair] * 2, name="join",
+                          compiler_params=pltpu.CompilerParams(vmem_limit_bytes=8 * 2**20))(*blocks)
+
+
+def near_pairs(own):
     ahead = moved(own, 1, 0, 0)
     behind = moved(own, -1, 0, 0)
     flip = moved(own, 0, 1, 0)
-    return both_cores([own, flip, ahead, behind])
-
-
-def far_blocks(near):
-    own, _, ahead, _ = near[:4]
-    across = moved(ahead, 1, 0, 0)
-    flip_ahead = moved(own, 1, 1, 0)
-    flip_behind = moved(own, -1, 1, 0)
-    flip_across = moved(ahead, 1, 1, 0)
-    return [across, flip_ahead, flip_behind, flip_across]
-
-
-def both_cores(mine):
-    return mine + [moved(block, 0, 0, 1) for block in mine]
+    return join(own, ahead, behind, flip)
+
+
+def far_pairs(near):
+    first, second = near
+    return [moved(second, -1, 0, 0), moved(first, 1, 1, 0)]
+
+
+def both_cores(pairs):
+    return list(pairs) + [moved(pair, 0, 0, 1) for pair in pairs]
 
 
 def body(ground_rows, best, cand_index, chosen_index):
@@ -319,20 +322,20 @@
     total = cand_index.shape[0]
     first_rows = total * 13 // 32
 
-    def finish(turn, limit, counts, rank, gains, level, blocks):
+    def finish(turn, limit, counts, rank, gains, level, pairs):
         state = jnp.stack([turn, limit]).astype(I32)
-        return gain(state, counts, cand, rank, gains, level, ground_rows, blocks, peers // 2,
+        return gain(state, counts, cand, rank, gains, level, ground_rows, pairs, peers // 2,
                     total - first_rows, chosen.shape[1], scale)
 
     block, rank, counts = pick(jnp.zeros((1,), I32), cand, chosen, ground_rows)
     turns = counts[2, 0]
-    near = near_blocks(block)
-    far = far_blocks(near)
+    near = near_pairs(block)
+    far = far_pairs(near)
+    near = both_cores(near)
     gains = gain(jnp.zeros((2,), I32), counts, cand, rank, jnp.zeros(cand.shape, F32), level, ground_rows, near,
                  0, first_rows, 0, scale)
     gains, far = lax.optimization_barrier((gains, far))
-    far = both_cores(far)
-    gains, new = finish(jnp.int32(0), jnp.int32(first_rows), counts, rank, gains, level, near + far)
+    gains, new = finish(jnp.int32(0), jnp.int32(first_rows), counts, rank, gains, level, near + both_cores(far))
 
     def more(state):
         return state[0] < turns
@@ -340,8 +343,9 @@
     def again(state):
         turn, gains, new = state
         block, rank, counts = pick(turn.reshape(1), cand, chosen, ground_rows)
-        near = near_blocks(block)
-        added, raised = finish(turn, jnp.int32(0), counts, rank, gains, level, near + both_cores(far_blocks(near)))
+        near = near_pairs(block)
+        pairs = both_cores(near) + both_cores(far_pairs(near))
+        added, raised = finish(turn, jnp.int32(0), counts, rank, gains, level, pairs)
         return turn + 1, added, jnp.maximum(new, raised)
 
     _, gains, new = lax.while_loop(more, again, (jnp.int32(1), gains, new))

time: 68.1 us -> 68.6 us (level)
  starting transfers between devices: 17.2 us -> 11.4 us
  Pallas kernels: 32.9 us -> 36.7 us
  waiting for transfers between devices: 6.49 us -> 9.4 us
    ppermute x15 -> x9, starting transfers between devices: 17.2 us -> 11.4 us  [moved(): return lax.ppermute(array, 'ground', pairs)]
    pallas_call x2, Pallas kernels: 26.8 us -> 30.5 us  [gain(): pl.pallas_call(body, in_specs=[pl.BlockSpec(memory_space=pltpu.SMEM)] * 2...]
    ppermute x15 -> x9, waiting for transfers between devices: 6.49 us -> 9.4 us  [moved(): return lax.ppermute(array, 'ground', pairs)]
  transfers between devices with their start and end apart: 15 -> 9, of which waited for: 6 -> 8; matrix products, arithmetic and copies ran while one was open for 1% -> 1% of each run, Pallas kernels for 16% -> 15%
where the time goes in v1:
time: 68.6 us; the launch traced here: 68.4 us
  Pallas kernels  36.7 us (53%)
  starting transfers between devices  11.4 us (17%)
  waiting for transfers between devices  9.4 us (14%)
  blocking collectives  8.32 us (12%)
  between operations  0.74 us (1%)
    pallas_call x2, Pallas kernels, gain(): pl.pallas_call(body, in_specs=[pl.BlockSpec(memory_space=pltpu.SMEM)] * 2...  30.5 us
    ppermute x9, starting transfers between devices, moved(): return lax.ppermute(array, 'ground', pairs)  11.4 us
    ppermute x9, waiting for transfers between devices, moved(): return lax.ppermute(array, 'ground', pairs)  9.4 us
    all_to_all x1, blocking collectives, body(): arrived = lax.all_to_all(blocks, 'ground', 0, 0, tiled=True)  8.32 us
    pallas_call x1, Pallas kernels, pick(): pl.pallas_call(pick_kernel, in_specs=[pl.BlockSpec(memory_space=pltpu.SME...  6.13 us
  transfers between devices with their start and end apart: 9, of which 8 were waited for; matrix products, arithmetic and copies ran while one was open for 1% of the time, Pallas kernels for 15%

profile of v1, /device:TPU:1, one launch (start us, length us, event | category | flops | bytes accessed | tf_op | source)
XLA Modules:
  0.0 68.4 jit_solution(3839206904686823954)
XLA Ops:
  0.7 6.1 %pick.2 = (bf16[112,1024]{1,0:T(8,128)(2,1)S(1)}, s32[8,128]{1,0:T(8,128)S(1)}, s32[8,128]{1,0:T(8,128)S(1)}) custom-call(s32[1]{0:T(128)} %constant.4.clone.1.turn_ref, s32[8,128]{1,0:T(8,128)} %bitcast.9, s32[1,64]{1,0:T(1,128)} %bitcast.13, bf16[8192,1024]{1,0:T(8,128)(2,1)} %refs_6_.3), custom_call_target="tpu_custom_call" | custom-call | tf_op jit(solution)/shard_map/pick/pallas_call | solution.py:102
  6.8 2.7 %collective-permute-start.11 = (bf16[112,1024]{1,0:T(8,128)(2,1)S(1)}, bf16[112,1024]{1,0:T(8,128)(2,1)S(1)}, u32[]{:S(2)}, u32[]{:S(2)}) collective-permute-start(bf16[112,1024]{1,0:T(8,128)(2,1)S(1)} %get-tuple-element.65.own_ref), channel_id=1, source_target_pairs={{0,2},{1,3},{2,0},{3,1},{4,6},{5,7},{6,4},{7,5},{8,10},{9,11},{10,... | collective-permute-start | bytes 688136 | tf_op jit(solution)/shard_map/ppermute | solution.py:270
  9.5 0.5 collective-permute-start.10
  10.0 2.2 %collective-permute-start.9 = (bf16[112,1024]{1,0:T(8,128)(2,1)S(1)}, bf16[112,1024]{1,0:T(8,128)(2,1)S(1)}, u32[]{:S(2)}, u32[]{:S(2)}) collective-permute-start(bf16[112,1024]{1,0:T(8,128)(2,1)S(1)} %get-tuple-element.65.own_ref), channel_id=1, source_target_pairs={{0,4},{1,13},{2,6},{3,15},{4,8},{5,1},{6,10},{7,3},{8,12},{9,5},{1... | collective-permute-start | bytes 688136 | tf_op jit(solution)/shard_map/ppermute | solution.py:270
  12.2 2.7 %collective-permute-done.11.flip_ref = bf16[112,1024]{1,0:T(8,128)(2,1)S(1)} collective-permute-done((bf16[112,1024]{1,0:T(8,128)(2,1)S(1)}, bf16[112,1024]{1,0:T(8,128)(2,1)S(1)}, u32[]{:S(2)}, u32[]{:S(2)}) %collective-permute-start.11) | collective-permute-done | bytes 229408 | tf_op jit(solution)/shard_map/ppermute | solution.py:270
  14.9 0.7 %collective-permute-done.10.behind_ref = bf16[112,1024]{1,0:T(8,128)(2,1)S(1)} collective-permute-done((bf16[112,1024]{1,0:T(8,128)(2,1)S(1)}, bf16[112,1024]{1,0:T(8,128)(2,1)S(1)}, u32[]{:S(2)}, u32[]{:S(2)}) %collective-permute-start.10) | collective-permute-done | bytes 229408 | tf_op jit(solution)/shard_map/ppermute | solution.py:270
  15.6 1.2 %collective-permute-done.9.ahead_ref = bf16[112,1024]{1,0:T(8,128)(2,1)S(1)} collective-permute-done((bf16[112,1024]{1,0:T(8,128)(2,1)S(1)}, bf16[112,1024]{1,0:T(8,128)(2,1)S(1)}, u32[]{:S(2)}, u32[]{:S(2)}) %collective-permute-start.9) | collective-permute-done | bytes 229408 | tf_op jit(solution)/shard_map/ppermute | solution.py:270
  16.9 3.5 %collective-permute-start.12 = (bf16[224,1024]{1,0:T(8,128)(2,1)S(1)}, bf16[224,1024]{1,0:T(8,128)(2,1)S(1)}, u32[]{:S(2)}, u32[]{:S(2)}) collective-permute-start(bf16[224,1024]{1,0:T(8,128)(2,1)S(1)} %get-tuple-element.66.refs_7_), channel_id=1, source_target_pairs={{0,1},{1,0},{2,3},{3,2},{4,5},{5,4},{6,7},{7,6},{8,9},{9,8},{10,11... | collective-permute-start | bytes 1376264 | tf_op jit(solution)/shard_map/ppermute | solution.py:270
  20.4 0.1 collective-permute-start.13
  20.5 1.0 %collective-permute-start.15 = (bf16[224,1024]{1,0:T(8,128)(2,1)S(1)}, bf16[224,1024]{1,0:T(8,128)(2,1)S(1)}, u32[]{:S(2)}, u32[]{:S(2)}) collective-permute-start(bf16[224,1024]{1,0:T(8,128)(2,1)S(1)} %get-tuple-element.66.refs_7_), channel_id=1, source_target_pairs={{0,6},{1,15},{2,4},{3,13},{4,10},{5,3},{6,8},{7,1},{8,14},{9,7},{1... | collective-permute-start | bytes 1376264 | tf_op jit(solution)/shard_map/ppermute | solution.py:270
  21.5 0.4 collective-permute-start.14
  21.9 0.6 collective-permute-done.13.refs_10_
  22.5 10.0 %gain.1.refs_4_ = f32[8,128]{1,0:T(8,128)S(1)} custom-call(s32[2]{0:T(128)S(1)} %broadcast_1_refs_0_.2.refs_0_, s32[8,128]{1,0:T(8,128)S(1)} %get-tuple-element.63.refs_1_, s32[8,128]{1,0:T(8,128)S(1)} %bitcast.10, s32[8,128]{1,0:T(8,128)S(1)} %get-tuple-element.64.refs_3_, f32[8,128]{1,0:T(8,128)S(1)} %broadcast_in_dim.3.refs_4_, f32[64,128]{1,0:T(8,128)S(1)} %bitcast.15, ...), custom_call_target="tpu_custom_call" | custom-call | flops 6979321856 | bytes 16777216 | tf_op jit(solution)/shard_map/gain/pallas_call | solution.py:247
  32.5 1.0 %collective-permute-done.15.refs_12_ = bf16[224,1024]{1,0:T(8,128)(2,1)S(1)} collective-permute-done((bf16[224,1024]{1,0:T(8,128)(2,1)S(1)}, bf16[224,1024]{1,0:T(8,128)(2,1)S(1)}, u32[]{:S(2)}, u32[]{:S(2)}) %collective-permute-start.15) | collective-permute-done | bytes 458784 | tf_op jit(solution)/shard_map/ppermute | solution.py:270
  33.5 1.6 %collective-permute-done.14.refs_11_ = bf16[224,1024]{1,0:T(8,128)(2,1)S(1)} collective-permute-done((bf16[224,1024]{1,0:T(8,128)(2,1)S(1)}, bf16[224,1024]{1,0:T(8,128)(2,1)S(1)}, u32[]{:S(2)}, u32[]{:S(2)}) %collective-permute-start.14) | collective-permute-done | bytes 458784 | tf_op jit(solution)/shard_map/ppermute | solution.py:270
  35.1 1.0 %collective-permute-start.16 = (bf16[224,1024]{1,0:T(8,128)(2,1)S(1)}, bf16[224,1024]{1,0:T(8,128)(2,1)S(1)}, u32[]{:S(2)}, u32[]{:S(2)}) collective-permute-start(bf16[224,1024]{1,0:T(8,128)(2,1)S(1)} %collective-permute-done.14.refs_11_), channel_id=1, source_target_pairs={{0,1},{1,0},{2,3},{3,2},{4,5},{5,4},{6,7},{7,6},{8,9},{9,8},{10,11... | collective-permute-start | bytes 1376264 | tf_op jit(solution)/shard_map/ppermute | solution.py:270
  36.1 0.5 slice.3
  36.6 0.9 %collective-permute-done.16.refs_13_ = bf16[224,1024]{1,0:T(8,128)(2,1)S(1)} collective-permute-done((bf16[224,1024]{1,0:T(8,128)(2,1)S(1)}, bf16[224,1024]{1,0:T(8,128)(2,1)S(1)}, u32[]{:S(2)}, u32[]{:S(2)}) %collective-permute-start.16) | collective-permute-done | bytes 458784 | tf_op jit(solution)/shard_map/ppermute | solution.py:270
  37.5 0.8 %collective-permute-done.17.refs_14_ = bf16[224,1024]{1,0:T(8,128)(2,1)} collective-permute-done((bf16[224,1024]{1,0:T(8,128)(2,1)S(1)}, bf16[224,1024]{1,0:T(8,128)(2,1)}, u32[]{:S(2)}, u32[]{:S(2)}) %collective-permute-start.17) | collective-permute-done | bytes 458784 | tf_op jit(solution)/shard_map/ppermute | solution.py:270
  38.3 20.4 %gain_last.2 = (f32[8,128]{1,0:T(8,128)S(1)}, f32[64,128]{1,0:T(8,128)S(1)}) custom-call(s32[2]{0:T(128)S(1)} %iota_multiply_fusion.refs_0_, s32[8,128]{1,0:T(8,128)S(1)} %get-tuple-element.63.refs_1_, s32[8,128]{1,0:T(8,128)S(1)} %bitcast.11, s32[8,128]{1,0:T(8,128)S(1)} %get-tuple-element.64.refs_3_, f32[8,128]{1,0:T(8,128)S(1)} %gain.1.refs_4_, ...), custom_call_target="tpu_custom_call" | custom-call | flops 11274289152 | bytes 16777216 | tf_op jit(solution)/shard_map/gain_last/pallas_call | solution.py:247
  58.7 0.7 while.12
  59.4 0.1 div.10
  59.5 8.3 %all_to_all.6 = f32[16,1,64]{2,1,0:T(1,128)S(1)} all-to-all(f32[16,1,64]{2,1,0:T(1,128)S(1)} %div.10), channel_id=1, replica_groups=mesh['cand'=8,'ground'=16] {'ground'}, dimensions={0} | all-to-all | bytes 8192 | tf_op jit(solution)/shard_map/all_to_all | solution.py:353
  67.8 0.5 reduce_sum.9
  (17 shorter events, 0.1 us)
Async XLA Ops:
  0.6 21.8 %copy-start = (bf16[8192,1024]{1,0:T(8,128)(2,1)S(1)}, bf16[8192,1024]{1,0:T(8,128)(2,1)}, u32[]{:S(2)}) copy-start(bf16[8192,1024]{1,0:T(8,128)(2,1)} %refs_6_.3) | copy-start | bytes 50331652
  0.6 21.8 %copy-start.2 = (s32[1024]{0:T(1024)S(1)}, s32[1024]{0:T(1024)}, u32[]{:S(2)}) copy-start(s32[1024]{0:T(1024)} %param.8) | copy-start | bytes 12292
  0.7 21.8 %copy-start.4 = (f32[8192]{0:T(1024)S(1)}, f32[8192]{0:T(1024)}, u32[]{:S(2)}) copy-start(f32[8192]{0:T(1024)} %param.7) | copy-start | bytes 98308
  6.8 8.1 %collective-permute-start.11 = (bf16[112,1024]{1,0:T(8,128)(2,1)S(1)}, bf16[112,1024]{1,0:T(8,128)(2,1)S(1)}, u32[]{:S(2)}, u32[]{:S(2)}) collective-permute-start(bf16[112,1024]{1,0:T(8,128)(2,1)S(1)} %get-tuple-element.65.own_ref), channel_id=1, source_target_pairs={{0,2},{1,3},{2,0},{3,1},{4,6},{5,7},{6,4},{7,5},{8,10},{9,11},{10,... | collective-permute-start | bytes 688136 | tf_op jit(solution)/shard_map/ppermute | solution.py:270
  9.5 6.1 %collective-permute-start.10 = (bf16[112,1024]{1,0:T(8,128)(2,1)S(1)}, bf16[112,1024]{1,0:T(8,128)(2,1)S(1)}, u32[]{:S(2)}, u32[]{:S(2)}) collective-permute-start(bf16[112,1024]{1,0:T(8,128)(2,1)S(1)} %get-tuple-element.65.own_ref), channel_id=1, source_target_pairs={{0,12},{1,5},{2,14},{3,7},{4,0},{5,9},{6,2},{7,11},{8,4},{9,13},{1... | collective-permute-start | bytes 688136 | tf_op jit(solution)/shard_map/ppermute | solution.py:270
  10.0 6.8 %collective-permute-start.9 = (bf16[112,1024]{1,0:T(8,128)(2,1)S(1)}, bf16[112,1024]{1,0:T(8,128)(2,1)S(1)}, u32[]{:S(2)}, u32[]{:S(2)}) collective-permute-start(bf16[112,1024]{1,0:T(8,128)(2,1)S(1)} %get-tuple-element.65.own_ref), channel_id=1, source_target_pairs={{0,4},{1,13},{2,6},{3,15},{4,8},{5,1},{6,10},{7,3},{8,12},{9,5},{1... | collective-permute-start | bytes 688136 | tf_op jit(solution)/shard_map/ppermute | solution.py:270
  16.9 5.0 %collective-permute-start.12 = (bf16[224,1024]{1,0:T(8,128)(2,1)S(1)}, bf16[224,1024]{1,0:T(8,128)(2,1)S(1)}, u32[]{:S(2)}, u32[]{:S(2)}) collective-permute-start(bf16[224,1024]{1,0:T(8,128)(2,1)S(1)} %get-tuple-element.66.refs_7_), channel_id=1, source_target_pairs={{0,1},{1,0},{2,3},{3,2},{4,5},{5,4},{6,7},{7,6},{8,9},{9,8},{10,11... | collective-permute-start | bytes 1376264 | tf_op jit(solution)/shard_map/ppermute | solution.py:270
  20.4 2.1 %collective-permute-start.13 = (bf16[224,1024]{1,0:T(8,128)(2,1)S(1)}, bf16[224,1024]{1,0:T(8,128)(2,1)S(1)}, u32[]{:S(2)}, u32[]{:S(2)}) collective-permute-start(bf16[224,1024]{1,0:T(8,128)(2,1)S(1)} %get-tuple-element.67.refs_8_), channel_id=1, source_target_pairs={{0,1},{1,0},{2,3},{3,2},{4,5},{5,4},{6,7},{7,6},{8,9},{9,8},{10,11... | collective-permute-start | bytes 1376264 | tf_op jit(solution)/shard_map/ppermute | solution.py:270
  20.5 13.0 %collective-permute-start.15 = (bf16[224,1024]{1,0:T(8,128)(2,1)S(1)}, bf16[224,1024]{1,0:T(8,128)(2,1)S(1)}, u32[]{:S(2)}, u32[]{:S(2)}) collective-permute-start(bf16[224,1024]{1,0:T(8,128)(2,1)S(1)} %get-tuple-element.66.refs_7_), channel_id=1, source_target_pairs={{0,6},{1,15},{2,4},{3,13},{4,10},{5,3},{6,8},{7,1},{8,14},{9,7},{1... | collective-permute-start | bytes 1376264 | tf_op jit(solution)/shard_map/ppermute | solution.py:270
  21.5 13.6 %collective-permute-start.14 = (bf16[224,1024]{1,0:T(8,128)(2,1)S(1)}, bf16[224,1024]{1,0:T(8,128)(2,1)S(1)}, u32[]{:S(2)}, u32[]{:S(2)}) collective-permute-start(bf16[224,1024]{1,0:T(8,128)(2,1)S(1)} %get-tuple-element.67.refs_8_), channel_id=1, source_target_pairs={{0,12},{1,5},{2,14},{3,7},{4,0},{5,9},{6,2},{7,11},{8,4},{9,13},{1... | collective-permute-start | bytes 1376264 | tf_op jit(solution)/shard_map/ppermute | solution.py:270
  35.1 2.4 %collective-permute-start.16 = (bf16[224,1024]{1,0:T(8,128)(2,1)S(1)}, bf16[224,1024]{1,0:T(8,128)(2,1)S(1)}, u32[]{:S(2)}, u32[]{:S(2)}) collective-permute-start(bf16[224,1024]{1,0:T(8,128)(2,1)S(1)} %collective-permute-done.14.refs_11_), channel_id=1, source_target_pairs={{0,1},{1,0},{2,3},{3,2},{4,5},{5,4},{6,7},{7,6},{8,9},{9,8},{10,11... | collective-permute-start | bytes 1376264 | tf_op jit(solution)/shard_map/ppermute | solution.py:270
  36.1 2.2 %collective-permute-start.17 = (bf16[224,1024]{1,0:T(8,128)(2,1)S(1)}, bf16[224,1024]{1,0:T(8,128)(2,1)}, u32[]{:S(2)}, u32[]{:S(2)}) collective-permute-start(bf16[224,1024]{1,0:T(8,128)(2,1)S(1)} %collective-permute-done.15.refs_12_), channel_id=1, source_target_pairs={{0,1},{1,0},{2,3},{3,2},{4,5},{5,4},{6,7},{7,6},{8,9},{9,8},{10,11... | collective-permute-start | bytes 1376264 | tf_op jit(solution)/shard_map/ppermute | solution.py:270
  36.6 22.2 %copy-start.3 = (s32[64]{0:T(128)S(1)}, s32[64]{0:T(128)}, u32[]{:S(2)}) copy-start(s32[64]{0:T(128)} %param.9) | copy-start | bytes 772
  59.4 9.0 %copy-start.1 = (f32[64,128]{1,0:T(8,128)}, f32[64,128]{1,0:T(8,128)S(1)}, u32[]{:S(2)}) copy-start(f32[64,128]{1,0:T(8,128)S(1)} %get-tuple-element.74) | copy-start | bytes 98308

commit v2 on v1

--- a/solution.py
+++ b/solution.py
@@ -113,15 +113,15 @@
     )(turn, cand, chosen, slab)
 
 
-def gain_kernel(turn_ref, counts_ref, cand_ref, rank_ref, before_ref, best_ref, slab_ref, *rest,
+def gain_kernel(turn_ref, counts_ref, cand_ref, rank_ref, before_ref, best_ref, floor_ref, slab_ref, *rest,
                 peers, earlier, main, last, scale):
     pairs = rest[: peers // 2]
     rest = rest[peers // 2 :]
     if last:
+        out_ref, level_ref, dense_ref, acc_ref, tall_ref, sems = rest
+    else:
         out_ref, level_ref, dense_ref, acc_ref = rest
-    else:
-        out_ref, dense_ref, acc_ref = rest
-        level_ref = None
+        level_ref[...] = floor_ref[...]
     count, _ = slab_ref.shape
     chunk = min(2048, count)
     chunks = count // chunk
@@ -129,6 +129,13 @@
     total = cand_ref.shape[0] * cand_ref.shape[1]
     head = dense_ref.shape[0] - 2 * SLOTS - (total if last else main)
     turn = turn_ref[0]
+    tall = slab_ref
+    if last:
+        tall = tall_ref
+        for i in range(chunks):
+            part = pl.ds(i * chunk, chunk)
+            pltpu.make_async_copy(slab_ref.at[part, :], tall_ref.at[part, :], sems.at[i]).start()
+
     sources = arrivals()[:peers]
     start = jnp.int32(0)
     done = jnp.int32(0)
@@ -181,7 +188,7 @@
         level = best_ref[lines, :]
         scaled = level * (1.0 / scale)
         for u in tiles:
-            sims = lax.dot_general(dense_ref[pl.ds(first, size), :], slab_ref[pl.ds(pl.multiple_of(i * chunk + u * sub, sub), sub), :],
+            sims = lax.dot_general(dense_ref[pl.ds(first, size), :], tall[pl.ds(pl.multiple_of(i * chunk + u * sub, sub), sub), :],
                                    (((1,), (1,)), ((), ())), preferred_element_type=F32)
             skip = head if with_head else 0
             part = acc_ref[pl.ds(first + skip, size - skip), :]
@@ -191,10 +198,14 @@
                 part += jnp.maximum(cols[skip:] - scaled[k : k + 1, :], 0.0)
                 if with_head:
                     top = jnp.max(cols[:skip] + low, axis=0, keepdims=True) * scale
-                    level_ref[pl.ds(i * per + k, 1), :] = jnp.maximum(level[k : k + 1, :], top)
+                    line = pl.ds(i * per + k, 1)
+                    level_ref[line, :] = jnp.maximum(floor_ref[line, :], top)
             acc_ref[pl.ds(first + skip, size - skip), :] = part
 
     def main_step(i, carry):
+        if last:
+            part = pl.ds(pl.multiple_of(i * chunk, chunk), chunk)
+            pltpu.make_async_copy(slab_ref.at[part, :], tall_ref.at[part, :], sems.at[i]).wait()
         add_up(i, 0, head + main, last, range(chunk // sub))
         return carry
 
@@ -223,8 +234,8 @@
             def rest_step(k, carry):
                 lines = sub // LANES
                 edges = best_ref[pl.ds(k * lines, lines), :] * (1.0 / scale)
-                tall = slab_ref[pl.ds(pl.multiple_of(k * sub, sub), sub), :]
-                sims = lax.dot_general(dense_ref[pl.ds(head + main, total - main), :], tall,
+                rows = tall[pl.ds(pl.multiple_of(k * sub, sub), sub), :]
+                sims = lax.dot_general(dense_ref[pl.ds(head + main, total - main), :], rows,
                                        (((1,), (1,)), ((), ())), preferred_element_type=F32)
                 for j in range(lines):
                     cols = sims[:, j * LANES : (j + 1) * LANES]
@@ -235,29 +246,31 @@
             hand_out(out_ref, main, total - main)
 
 
-def gain(turn, counts, cand, rank, before, best, slab, pairs, earlier, main, chosen, scale):
+def gain(turn, counts, cand, rank, before, best, floor, slab, pairs, earlier, main, chosen, scale):
     count, width = slab.shape
     total = cand.shape[0] * cand.shape[1]
     peers = 2 * len(pairs)
     last = chosen > 0
+    chunk = min(2048, count)
+    copies = [pltpu.VMEM(slab.shape, BF16), pltpu.SemaphoreType.DMA((count // chunk,))] * last
     body = lambda *refs: gain_kernel(*refs, peers=peers, earlier=earlier, main=main, last=last, scale=scale)
     vmem = pl.BlockSpec(memory_space=pltpu.VMEM)
-    outs = [jax.ShapeDtypeStruct(cand.shape, F32)] + [jax.ShapeDtypeStruct(best.shape, F32)] * last
+    outs = [jax.ShapeDtypeStruct(cand.shape, F32), jax.ShapeDtypeStruct(best.shape, F32)]
     rows = chosen + (total if last else main)
-    made = pl.pallas_call(
+    return pl.pallas_call(
         body,
-        in_specs=[pl.BlockSpec(memory_space=pltpu.SMEM)] * 2 + [vmem] * 4
-        + [vmem] + [vmem] * len(pairs),
+        in_specs=[pl.BlockSpec(memory_space=pltpu.SMEM)] * 2 + [vmem] * 5
+        + [pl.BlockSpec(memory_space=pl.ANY) if last else vmem] + [vmem] * len(pairs),
         out_specs=[vmem] * len(outs),
         out_shape=outs,
         scratch_shapes=[pltpu.VMEM((rows + 2 * SLOTS, width), BF16),
-                        pltpu.VMEM((rows, LANES), F32)],
-        compiler_params=pltpu.CompilerParams(vmem_limit_bytes=24 * 2**20),
+                        pltpu.VMEM((rows, LANES), F32),
+                        *copies],
+        compiler_params=pltpu.CompilerParams(vmem_limit_bytes=(40 if last else 24) * 2**20),
         cost_estimate=pl.CostEstimate(flops=2 * count * width * (main + chosen), transcendentals=0,
                                       bytes_accessed=2 * count * width),
         name="gain_last" if last else "gain",
-    )(turn, counts, cand, rank, before, best, slab, *pairs)
-    return made if last else made[0]
+    )(turn, counts, cand, rank, before, best, floor, slab, *pairs)
 
 
 def device(x, y, c):
@@ -320,11 +333,11 @@
     chosen = chosen_index.reshape(1, -1)
     level = best.reshape(-1, LANES)
     total = cand_index.shape[0]
-    first_rows = total * 13 // 32
-
-    def finish(turn, limit, counts, rank, gains, level, pairs):
+    first_rows = total * 7 // 16
+
+    def finish(turn, limit, counts, rank, gains, floor, pairs):
         state = jnp.stack([turn, limit]).astype(I32)
-        return gain(state, counts, cand, rank, gains, level, ground_rows, pairs, peers // 2,
+        return gain(state, counts, cand, rank, gains, level, floor, ground_rows, pairs, peers // 2,
                     total - first_rows, chosen.shape[1], scale)
 
     block, rank, counts = pick(jnp.zeros((1,), I32), cand, chosen, ground_rows)
@@ -332,8 +345,8 @@
     near = near_pairs(block)
     far = far_pairs(near)
     near = both_cores(near)
-    gains = gain(jnp.zeros((2,), I32), counts, cand, rank, jnp.zeros(cand.shape, F32), level, ground_rows, near,
-                 0, first_rows, 0, scale)
+    gains, unused = gain(jnp.zeros((2,), I32), counts, cand, rank, jnp.zeros(cand.shape, F32), level, level,
+                      ground_rows, near, 0, first_rows, 0, scale)
     gains, far = lax.optimization_barrier((gains, far))
     gains, new = finish(jnp.int32(0), jnp.int32(first_rows), counts, rank, gains, level, near + both_cores(far))
 
@@ -345,10 +358,10 @@
         block, rank, counts = pick(turn.reshape(1), cand, chosen, ground_rows)
         near = near_pairs(block)
         pairs = both_cores(near) + both_cores(far_pairs(near))
-        added, raised = finish(turn, jnp.int32(0), counts, rank, gains, level, pairs)
-        return turn + 1, added, jnp.maximum(new, raised)
-
-    _, gains, new = lax.while_loop(more, again, (jnp.int32(1), gains, new))
+        gains, new = finish(turn, jnp.int32(0), counts, rank, gains, new, pairs)
+        return turn + 1, gains, new
+
+    unused, gains, new = lax.while_loop(more, again, (jnp.int32(1), gains, new))
     blocks = gains.reshape(peers, -1) / whole
     arrived = lax.all_to_all(blocks, "ground", 0, 0, tiled=True)
     return arrived.sum(axis=0), new.reshape(-1)

time: 68.6 us -> 63.5 us (0.926)
  Pallas kernels: 36.7 us -> 32.4 us
  waiting for transfers between devices: 9.4 us -> 8.57 us
    pallas_call x2, Pallas kernels: 30.5 us -> 26.2 us  [gain(): pl.pallas_call(body, in_specs=[pl.BlockSpec(memory_space=pltpu.SMEM)] * 2...]
    ppermute x9, waiting for transfers between devices: 9.4 us -> 8.57 us  [moved(): return lax.ppermute(array, 'ground', pairs)]
  transfers between devices with their start and end apart: 9 -> 9, of which waited for: 8 -> 8; matrix products, arithmetic and copies ran while one was open for 1% -> 1% of each run, Pallas kernels for 15% -> 17%
where the time goes in v2:
time: 63.5 us; the launch traced here: 63.3 us
  Pallas kernels  32.4 us (51%)
  starting transfers between devices  11.4 us (18%)
  waiting for transfers between devices  8.57 us (13%)
  blocking collectives  8.33 us (13%)
  between operations  0.73 us (1%)
  loops' own time  0.65 us (1%)
    pallas_call x2, Pallas kernels, gain(): pl.pallas_call(body, in_specs=[pl.BlockSpec(memory_space=pltpu.SMEM)] * 2...  26.2 us
    ppermute x9, starting transfers between devices, moved(): return lax.ppermute(array, 'ground', pairs)  11.4 us
    ppermute x9, waiting for transfers between devices, moved(): return lax.ppermute(array, 'ground', pairs)  8.57 us
    all_to_all x1, blocking collectives, body(): arrived = lax.all_to_all(blocks, 'ground', 0, 0, tiled=True)  8.33 us
    pallas_call x1, Pallas kernels, pick(): pl.pallas_call(pick_kernel, in_specs=[pl.BlockSpec(memory_space=pltpu.SME...  6.13 us
  transfers between devices with their start and end apart: 9, of which 8 were waited for; matrix products, arithmetic and copies ran while one was open for 1% of the time, Pallas kernels for 17%

profile of v2, /device:TPU:1, one launch (start us, length us, event | category | flops | bytes accessed | tf_op | source)
XLA Modules:
  0.0 63.3 jit_solution(11177069683352536694)
XLA Ops:
  0.7 6.1 %pick.2 = (bf16[112,1024]{1,0:T(8,128)(2,1)S(1)}, s32[8,128]{1,0:T(8,128)S(1)}, s32[8,128]{1,0:T(8,128)S(1)}) custom-call(s32[1]{0:T(128)} %constant.4.clone.1.turn_ref, s32[8,128]{1,0:T(8,128)} %bitcast.9, s32[1,64]{1,0:T(1,128)} %bitcast.13, bf16[8192,1024]{1,0:T(8,128)(2,1)} %refs_7_.3), custom_call_target="tpu_custom_call" | custom-call | tf_op jit(solution)/shard_map/pick/pallas_call | solution.py:102
  6.8 2.7 %collective-permute-start.11 = (bf16[112,1024]{1,0:T(8,128)(2,1)S(1)}, bf16[112,1024]{1,0:T(8,128)(2,1)S(1)}, u32[]{:S(2)}, u32[]{:S(2)}) collective-permute-start(bf16[112,1024]{1,0:T(8,128)(2,1)S(1)} %get-tuple-element.66.own_ref), channel_id=1, source_target_pairs={{0,2},{1,3},{2,0},{3,1},{4,6},{5,7},{6,4},{7,5},{8,10},{9,11},{10,... | collective-permute-start | bytes 688136 | tf_op jit(solution)/shard_map/ppermute | solution.py:283
  9.5 0.5 collective-permute-start.10
  10.0 2.2 %collective-permute-start.9 = (bf16[112,1024]{1,0:T(8,128)(2,1)S(1)}, bf16[112,1024]{1,0:T(8,128)(2,1)S(1)}, u32[]{:S(2)}, u32[]{:S(2)}) collective-permute-start(bf16[112,1024]{1,0:T(8,128)(2,1)S(1)} %get-tuple-element.66.own_ref), channel_id=1, source_target_pairs={{0,4},{1,13},{2,6},{3,15},{4,8},{5,1},{6,10},{7,3},{8,12},{9,5},{1... | collective-permute-start | bytes 688136 | tf_op jit(solution)/shard_map/ppermute | solution.py:283
  12.2 2.7 %collective-permute-done.11.flip_ref = bf16[112,1024]{1,0:T(8,128)(2,1)S(1)} collective-permute-done((bf16[112,1024]{1,0:T(8,128)(2,1)S(1)}, bf16[112,1024]{1,0:T(8,128)(2,1)S(1)}, u32[]{:S(2)}, u32[]{:S(2)}) %collective-permute-start.11) | collective-permute-done | bytes 229408 | tf_op jit(solution)/shard_map/ppermute | solution.py:283
  14.9 0.7 %collective-permute-done.10.behind_ref = bf16[112,1024]{1,0:T(8,128)(2,1)S(1)} collective-permute-done((bf16[112,1024]{1,0:T(8,128)(2,1)S(1)}, bf16[112,1024]{1,0:T(8,128)(2,1)S(1)}, u32[]{:S(2)}, u32[]{:S(2)}) %collective-permute-start.10) | collective-permute-done | bytes 229408 | tf_op jit(solution)/shard_map/ppermute | solution.py:283
  15.6 1.2 %collective-permute-done.9.ahead_ref = bf16[112,1024]{1,0:T(8,128)(2,1)S(1)} collective-permute-done((bf16[112,1024]{1,0:T(8,128)(2,1)S(1)}, bf16[112,1024]{1,0:T(8,128)(2,1)S(1)}, u32[]{:S(2)}, u32[]{:S(2)}) %collective-permute-start.9) | collective-permute-done | bytes 229408 | tf_op jit(solution)/shard_map/ppermute | solution.py:283
  16.9 3.5 %collective-permute-start.12 = (bf16[224,1024]{1,0:T(8,128)(2,1)S(1)}, bf16[224,1024]{1,0:T(8,128)(2,1)S(1)}, u32[]{:S(2)}, u32[]{:S(2)}) collective-permute-start(bf16[224,1024]{1,0:T(8,128)(2,1)S(1)} %get-tuple-element.67.refs_8_), channel_id=1, source_target_pairs={{0,1},{1,0},{2,3},{3,2},{4,5},{5,4},{6,7},{7,6},{8,9},{9,8},{10,11... | collective-permute-start | bytes 1376264 | tf_op jit(solution)/shard_map/ppermute | solution.py:283
  20.4 0.1 collective-permute-start.13
  20.5 1.0 %collective-permute-start.15 = (bf16[224,1024]{1,0:T(8,128)(2,1)S(1)}, bf16[224,1024]{1,0:T(8,128)(2,1)S(1)}, u32[]{:S(2)}, u32[]{:S(2)}) collective-permute-start(bf16[224,1024]{1,0:T(8,128)(2,1)S(1)} %get-tuple-element.67.refs_8_), channel_id=1, source_target_pairs={{0,6},{1,15},{2,4},{3,13},{4,10},{5,3},{6,8},{7,1},{8,14},{9,7},{1... | collective-permute-start | bytes 1376264 | tf_op jit(solution)/shard_map/ppermute | solution.py:283
  21.5 0.4 collective-permute-start.14
  21.9 0.6 collective-permute-done.13.refs_11_
  22.5 10.9 %gain.1 = (f32[8,128]{1,0:T(8,128)S(1)}, f32[64,128]{1,0:T(8,128)}) custom-call(s32[2]{0:T(128)S(1)} %broadcast_1_refs_0_.2.refs_0_, s32[8,128]{1,0:T(8,128)S(1)} %get-tuple-element.64.refs_1_, s32[8,128]{1,0:T(8,128)S(1)} %bitcast.10, s32[8,128]{1,0:T(8,128)S(1)} %get-tuple-element.65.refs_3_, f32[8,128]{1,0:T(8,128)S(1)} %broadcast_in_dim.3.refs_4_, ...), custom_call_target="tpu_custom_call" | custom-call | flops 7516192768 | bytes 16777216 | tf_op jit(solution)/shard_map/gain/pallas_call | solution.py:260
  33.4 0.1 collective-permute-done.15.refs_13_
  33.5 1.6 %collective-permute-done.14.refs_12_ = bf16[224,1024]{1,0:T(8,128)(2,1)S(1)} collective-permute-done((bf16[224,1024]{1,0:T(8,128)(2,1)S(1)}, bf16[224,1024]{1,0:T(8,128)(2,1)S(1)}, u32[]{:S(2)}, u32[]{:S(2)}) %collective-permute-start.14) | collective-permute-done | bytes 458784 | tf_op jit(solution)/shard_map/ppermute | solution.py:283
  35.1 1.0 %collective-permute-start.16 = (bf16[224,1024]{1,0:T(8,128)(2,1)S(1)}, bf16[224,1024]{1,0:T(8,128)(2,1)S(1)}, u32[]{:S(2)}, u32[]{:S(2)}) collective-permute-start(bf16[224,1024]{1,0:T(8,128)(2,1)S(1)} %collective-permute-done.14.refs_12_), channel_id=1, source_target_pairs={{0,1},{1,0},{2,3},{3,2},{4,5},{5,4},{6,7},{7,6},{8,9},{9,8},{10,11... | collective-permute-start | bytes 1376264 | tf_op jit(solution)/shard_map/ppermute | solution.py:283
  36.1 0.5 slice.3
  36.6 0.9 %collective-permute-done.16.refs_14_ = bf16[224,1024]{1,0:T(8,128)(2,1)S(1)} collective-permute-done((bf16[224,1024]{1,0:T(8,128)(2,1)S(1)}, bf16[224,1024]{1,0:T(8,128)(2,1)S(1)}, u32[]{:S(2)}, u32[]{:S(2)}) %collective-permute-start.16) | collective-permute-done | bytes 458784 | tf_op jit(solution)/shard_map/ppermute | solution.py:283
  37.5 0.8 %collective-permute-done.17.refs_15_ = bf16[224,1024]{1,0:T(8,128)(2,1)} collective-permute-done((bf16[224,1024]{1,0:T(8,128)(2,1)S(1)}, bf16[224,1024]{1,0:T(8,128)(2,1)}, u32[]{:S(2)}, u32[]{:S(2)}) %collective-permute-start.17) | collective-permute-done | bytes 458784 | tf_op jit(solution)/shard_map/ppermute | solution.py:283
  38.3 15.3 %gain_last.2 = (f32[8,128]{1,0:T(8,128)S(1)}, f32[64,128]{1,0:T(8,128)S(1)}) custom-call(s32[2]{0:T(128)S(1)} %iota_multiply_fusion.refs_0_, s32[8,128]{1,0:T(8,128)S(1)} %get-tuple-element.64.refs_1_, s32[8,128]{1,0:T(8,128)S(1)} %bitcast.11, s32[8,128]{1,0:T(8,128)S(1)} %get-tuple-element.65.refs_3_, f32[8,128]{1,0:T(8,128)S(1)} %get-tuple-element.70.refs_4_, ...), custom_call_target="tpu_custom_call" | custom-call | flops 10737418240 | bytes 16777216 | tf_op jit(solution)/shard_map/gain_last/pallas_call | solution.py:260
  53.6 0.7 %while.12 = (s32[]{:T(128)}, f32[8,128]{1,0:T(8,128)S(1)}, f32[64,128]{1,0:T(8,128)S(1)}, s32[]{:T(128)}, s32[8,128]{1,0:T(8,128)S(1)}, /*index=5*/s32[1,64]{1,0...) while((s32[]{:T(128)}, f32[8,128]{1,0:T(8,128)S(1)}, ...), condition=%wide.region_1.0_spmd, body=%wide.region_0.0_spmd.sunk | while | flops 10737418240 | bytes 30613988 | solution.py:364
  54.3 0.1 div.10
  54.4 8.3 %all_to_all.6 = f32[16,1,64]{2,1,0:T(1,128)S(1)} all-to-all(f32[16,1,64]{2,1,0:T(1,128)S(1)} %div.10), channel_id=1, replica_groups=mesh['cand'=8,'ground'=16] {'ground'}, dimensions={0} | all-to-all | bytes 8192 | tf_op jit(solution)/shard_map/all_to_all | solution.py:366
  62.7 0.5 reduce_sum.9
  (17 shorter events, 0.1 us)
Async XLA Ops:
  0.6 21.8 %copy-start = (bf16[8192,1024]{1,0:T(8,128)(2,1)S(1)}, bf16[8192,1024]{1,0:T(8,128)(2,1)}, u32[]{:S(2)}) copy-start(bf16[8192,1024]{1,0:T(8,128)(2,1)} %refs_7_.3) | copy-start | bytes 50331652
  0.6 21.8 %copy-start.2 = (s32[1024]{0:T(1024)S(1)}, s32[1024]{0:T(1024)}, u32[]{:S(2)}) copy-start(s32[1024]{0:T(1024)} %param.8) | copy-start | bytes 12292
  0.7 21.8 %copy-start.4 = (f32[8192]{0:T(1024)S(1)}, f32[8192]{0:T(1024)}, u32[]{:S(2)}) copy-start(f32[8192]{0:T(1024)} %param.7) | copy-start | bytes 98308
  6.8 8.1 %collective-permute-start.11 = (bf16[112,1024]{1,0:T(8,128)(2,1)S(1)}, bf16[112,1024]{1,0:T(8,128)(2,1)S(1)}, u32[]{:S(2)}, u32[]{:S(2)}) collective-permute-start(bf16[112,1024]{1,0:T(8,128)(2,1)S(1)} %get-tuple-element.66.own_ref), channel_id=1, source_target_pairs={{0,2},{1,3},{2,0},{3,1},{4,6},{5,7},{6,4},{7,5},{8,10},{9,11},{10,... | collective-permute-start | bytes 688136 | tf_op jit(solution)/shard_map/ppermute | solution.py:283
  9.5 6.1 %collective-permute-start.10 = (bf16[112,1024]{1,0:T(8,128)(2,1)S(1)}, bf16[112,1024]{1,0:T(8,128)(2,1)S(1)}, u32[]{:S(2)}, u32[]{:S(2)}) collective-permute-start(bf16[112,1024]{1,0:T(8,128)(2,1)S(1)} %get-tuple-element.66.own_ref), channel_id=1, source_target_pairs={{0,12},{1,5},{2,14},{3,7},{4,0},{5,9},{6,2},{7,11},{8,4},{9,13},{1... | collective-permute-start | bytes 688136 | tf_op jit(solution)/shard_map/ppermute | solution.py:283
  10.0 6.8 %collective-permute-start.9 = (bf16[112,1024]{1,0:T(8,128)(2,1)S(1)}, bf16[112,1024]{1,0:T(8,128)(2,1)S(1)}, u32[]{:S(2)}, u32[]{:S(2)}) collective-permute-start(bf16[112,1024]{1,0:T(8,128)(2,1)S(1)} %get-tuple-element.66.own_ref), channel_id=1, source_target_pairs={{0,4},{1,13},{2,6},{3,15},{4,8},{5,1},{6,10},{7,3},{8,12},{9,5},{1... | collective-permute-start | bytes 688136 | tf_op jit(solution)/shard_map/ppermute | solution.py:283
  16.9 5.0 %collective-permute-start.12 = (bf16[224,1024]{1,0:T(8,128)(2,1)S(1)}, bf16[224,1024]{1,0:T(8,128)(2,1)S(1)}, u32[]{:S(2)}, u32[]{:S(2)}) collective-permute-start(bf16[224,1024]{1,0:T(8,128)(2,1)S(1)} %get-tuple-element.67.refs_8_), channel_id=1, source_target_pairs={{0,1},{1,0},{2,3},{3,2},{4,5},{5,4},{6,7},{7,6},{8,9},{9,8},{10,11... | collective-permute-start | bytes 1376264 | tf_op jit(solution)/shard_map/ppermute | solution.py:283
  20.4 2.1 %collective-permute-start.13 = (bf16[224,1024]{1,0:T(8,128)(2,1)S(1)}, bf16[224,1024]{1,0:T(8,128)(2,1)S(1)}, u32[]{:S(2)}, u32[]{:S(2)}) collective-permute-start(bf16[224,1024]{1,0:T(8,128)(2,1)S(1)} %get-tuple-element.68.refs_9_), channel_id=1, source_target_pairs={{0,1},{1,0},{2,3},{3,2},{4,5},{5,4},{6,7},{7,6},{8,9},{9,8},{10,11... | collective-permute-start | bytes 1376264 | tf_op jit(solution)/shard_map/ppermute | solution.py:283
  20.5 13.0 %collective-permute-start.15 = (bf16[224,1024]{1,0:T(8,128)(2,1)S(1)}, bf16[224,1024]{1,0:T(8,128)(2,1)S(1)}, u32[]{:S(2)}, u32[]{:S(2)}) collective-permute-start(bf16[224,1024]{1,0:T(8,128)(2,1)S(1)} %get-tuple-element.67.refs_8_), channel_id=1, source_target_pairs={{0,6},{1,15},{2,4},{3,13},{4,10},{5,3},{6,8},{7,1},{8,14},{9,7},{1... | collective-permute-start | bytes 1376264 | tf_op jit(solution)/shard_map/ppermute | solution.py:283
  21.5 13.6 %collective-permute-start.14 = (bf16[224,1024]{1,0:T(8,128)(2,1)S(1)}, bf16[224,1024]{1,0:T(8,128)(2,1)S(1)}, u32[]{:S(2)}, u32[]{:S(2)}) collective-permute-start(bf16[224,1024]{1,0:T(8,128)(2,1)S(1)} %get-tuple-element.68.refs_9_), channel_id=1, source_target_pairs={{0,12},{1,5},{2,14},{3,7},{4,0},{5,9},{6,2},{7,11},{8,4},{9,13},{1... | collective-permute-start | bytes 1376264 | tf_op jit(solution)/shard_map/ppermute | solution.py:283
  35.1 2.4 %collective-permute-start.16 = (bf16[224,1024]{1,0:T(8,128)(2,1)S(1)}, bf16[224,1024]{1,0:T(8,128)(2,1)S(1)}, u32[]{:S(2)}, u32[]{:S(2)}) collective-permute-start(bf16[224,1024]{1,0:T(8,128)(2,1)S(1)} %collective-permute-done.14.refs_12_), channel_id=1, source_target_pairs={{0,1},{1,0},{2,3},{3,2},{4,5},{5,4},{6,7},{7,6},{8,9},{9,8},{10,11... | collective-permute-start | bytes 1376264 | tf_op jit(solution)/shard_map/ppermute | solution.py:283
  36.1 2.2 %collective-permute-start.17 = (bf16[224,1024]{1,0:T(8,128)(2,1)S(1)}, bf16[224,1024]{1,0:T(8,128)(2,1)}, u32[]{:S(2)}, u32[]{:S(2)}) collective-permute-start(bf16[224,1024]{1,0:T(8,128)(2,1)S(1)} %collective-permute-done.15.refs_13_), channel_id=1, source_target_pairs={{0,1},{1,0},{2,3},{3,2},{4,5},{5,4},{6,7},{7,6},{8,9},{9,8},{10,11... | collective-permute-start | bytes 1376264 | tf_op jit(solution)/shard_map/ppermute | solution.py:283
  36.6 17.0 %copy-start.3 = (s32[64]{0:T(128)S(1)}, s32[64]{0:T(128)}, u32[]{:S(2)}) copy-start(s32[64]{0:T(128)} %param.9) | copy-start | bytes 772
  54.3 9.0 %copy-start.1 = (f32[64,128]{1,0:T(8,128)}, f32[64,128]{1,0:T(8,128)S(1)}, u32[]{:S(2)}) copy-start(f32[64,128]{1,0:T(8,128)S(1)} %get-tuple-element.76) | copy-start | bytes 98308

commit v3 on v2

--- a/solution.py
+++ b/solution.py
@@ -6,9 +6,9 @@
 from jax.sharding import PartitionSpec as P
 
 
-CAP = 96
+SLOTS = 104
 CAP_CHOSEN = 16
-SLOTS = CAP + CAP_CHOSEN
+WINDOW = 2 * SLOTS + 16
 LANES = 128
 TILE = 8
 
@@ -19,6 +19,11 @@
 
 def iota(shape, dim):
     return lax.broadcasted_iota(I32, shape, dim)
+
+
+def sent_and_room(turn, chosen):
+    before = turn * CAP_CHOSEN
+    return SLOTS * turn - jnp.minimum(chosen, before), SLOTS - jnp.clip(chosen - before, 0, CAP_CHOSEN)
 
 
 def pick_kernel(turn_ref, cand_ref, chosen_ref, slab_ref, block_ref, rank_ref, counts_ref,
@@ -46,9 +51,11 @@
     ahead = jnp.concatenate(lines + [jnp.zeros((8, LANES), F32)], axis=0)
     slot = (upto - 1.0 + ahead).astype(I32)
     top = iota(index.shape, 0) < rows
-    slot = slot - turn * jnp.where(top, CAP, CAP_CHOSEN)
-    inside = mine & (slot >= 0) & (slot < jnp.where(top, CAP, CAP_CHOSEN))
-    slot = jnp.where(inside, jnp.where(top, slot, slot + CAP), -1)
+    chosen_here = upto[rows : rows + 1, LANES - 1 : LANES].astype(I32)
+    sent, room = sent_and_room(turn, chosen_here)
+    slot = slot - jnp.where(top, sent, turn * CAP_CHOSEN)
+    inside = mine & (slot >= 0) & (slot < jnp.where(top, room, CAP_CHOSEN))
+    slot = jnp.where(inside, jnp.where(top, slot, SLOTS - 1 - slot), -1)
     packed = jnp.where(inside, index - me * count, 0)
     slot_t = slot.T
     packed_t = packed.T
@@ -83,7 +90,7 @@
     rank_ref[...] = jnp.concatenate(ranks, axis=1).T.astype(I32)
     _, ccounts = ranked(index_t[:, rows : rows + 1], jnp.zeros((1, LANES), F32))
     turns = jnp.maximum(
-        (jnp.max(counts, axis=1, keepdims=True).astype(I32) + CAP - 1) // CAP,
+        (jnp.max(counts + ccounts, axis=1, keepdims=True).astype(I32) + SLOTS - 1) // SLOTS,
         (jnp.max(ccounts, axis=1, keepdims=True).astype(I32) + CAP_CHOSEN - 1) // CAP_CHOSEN,
     )
     counts_ref[0:1, :] = counts.astype(I32)
@@ -123,11 +130,11 @@
         out_ref, level_ref, dense_ref, acc_ref = rest
         level_ref[...] = floor_ref[...]
     count, _ = slab_ref.shape
-    chunk = min(2048, count)
+    chunk = min(2048 if last else 4096, count)
     chunks = count // chunk
     shift = count.bit_length() - 1
     total = cand_ref.shape[0] * cand_ref.shape[1]
-    head = dense_ref.shape[0] - 2 * SLOTS - (total if last else main)
+    head = dense_ref.shape[0] - WINDOW - (total if last else main)
     turn = turn_ref[0]
     tall = slab_ref
     if last:
@@ -139,12 +146,14 @@
     sources = arrivals()[:peers]
     start = jnp.int32(0)
     done = jnp.int32(0)
-    starts, heres = [], []
+    starts, heres, sents = [], [], []
     for a in range(peers):
         if a == earlier:
             done = jnp.minimum(start, turn_ref[1])
-        here = jnp.clip(counts_ref[0, sources[a]] - turn * CAP, 0, CAP)
+        sent, room = sent_and_room(turn, counts_ref[1, sources[a]])
+        here = jnp.clip(counts_ref[0, sources[a]] - sent, 0, room)
         starts.append(start)
+        sents.append(sent)
         heres.append(here)
         start = start + here
     stop = start if last else jnp.minimum(start, main)
@@ -152,19 +161,24 @@
     dense_ref[...] = jnp.zeros_like(dense_ref)
     acc_ref[...] = jnp.zeros_like(acc_ref)
     q = iota((1, 2 * SLOTS), 1)
+
+    def place_pair(a):
+        row = jnp.where(q < SLOTS, q + starts[a], q - SLOTS + starts[a + 1])
+        ends = jnp.where(q < SLOTS, starts[a] + heres[a], starts[a + 1] + heres[a + 1])
+        good = (row < ends) & (row >= done) & (row < stop)
+        target = jnp.where(good, row - done, -1)
+        bound = total if last else main
+        base = pl.multiple_of(jnp.clip(starts[a] - done, 0, bound) // 16 * 16, 16)
+        one = jnp.where(iota((WINDOW, 1), 0) + base == target, 1.0, 0.0).astype(BF16)
+        rows = jnp.dot(one, pairs[a // 2][...], preferred_element_type=F32)
+        window = pl.ds(pl.multiple_of(base + head, 16), WINDOW)
+        dense_ref[window, :] = (dense_ref[window, :].astype(F32) + rows).astype(BF16)
+
     for a in range(0, peers, 2):
-
-        @pl.when((starts[a] < stop) & (starts[a + 1] + heres[a + 1] > done))
-        def _():
-            row = jnp.where(q < SLOTS, q + starts[a], q - SLOTS + starts[a + 1])
-            ends = jnp.where(q < SLOTS, starts[a] + heres[a], starts[a + 1] + heres[a + 1])
-            good = (row < ends) & (row >= done) & (row < stop)
-            target = jnp.where(good, row - done, -1)
-            base = pl.multiple_of(jnp.maximum(starts[a] - done, 0) // 16 * 16, 16)
-            one = jnp.where(iota((2 * SLOTS, 1), 0) + base == target, 1.0, 0.0).astype(BF16)
-            rows = jnp.dot(one, pairs[a // 2][...], preferred_element_type=F32)
-            window = pl.ds(pl.multiple_of(base + head, 16), 2 * SLOTS)
-            dense_ref[window, :] = (dense_ref[window, :].astype(F32) + rows).astype(BF16)
+        if a < earlier:
+            pl.when(starts[a + 1] + heres[a + 1] > done)(lambda a=a: place_pair(a))
+        else:
+            place_pair(a)
 
     there = jnp.int32(0)
     if last:
@@ -172,11 +186,12 @@
         target = jnp.full((1, peers * CAP_CHOSEN), -1, I32)
         for a in range(peers):
             here = jnp.clip(counts_ref[1, sources[a]] - turn * CAP_CHOSEN, 0, CAP_CHOSEN)
-            slot = q - a * CAP_CHOSEN
-            target = jnp.where((slot >= 0) & (slot < here), slot + there, target)
+            slot = (a + 1) * CAP_CHOSEN - 1 - q
+            good = (slot >= 0) & (slot < here) & (slot < CAP_CHOSEN)
+            target = jnp.where(good, slot + there, target)
             there = there + here
         one = jnp.where(iota((head, 1), 0) == target, 1.0, 0.0).astype(BF16)
-        rows = jnp.concatenate([pairs[a // 2][a % 2 * SLOTS + CAP : a % 2 * SLOTS + SLOTS, :] for a in range(peers)], axis=0)
+        rows = jnp.concatenate([pairs[a // 2][(a % 2 + 1) * SLOTS - CAP_CHOSEN : (a % 2 + 1) * SLOTS, :] for a in range(peers)], axis=0)
         dense_ref[0:head, :] = jnp.dot(one, rows, preferred_element_type=F32).astype(BF16)
 
     sub = 256
@@ -212,17 +227,17 @@
     lax.fori_loop(0, chunks, main_step, 0)
 
     slab = lax.shift_right_arithmetic(cand_ref[...], shift)
-    slot = rank_ref[...] - turn * CAP
-    place = jnp.full(slot.shape, -1, I32)
+    place = jnp.full(slab.shape, -1, I32)
     for a in range(peers):
-        place = jnp.where(slab == sources[a], slot + starts[a] - done, place)
-    good = (slot >= 0) & (slot < CAP) & (place >= 0) & (place < stop - done)
-    place = jnp.where(good, place, -1)
+        slot = rank_ref[...] - sents[a]
+        good = (slab == sources[a]) & (slot >= 0) & (slot < heres[a])
+        place = jnp.where(good, slot + starts[a] - done, place)
+    place = jnp.where((place >= 0) & (place < stop - done), place, -1)
 
     def hand_out(ref, first, size):
         sums = jnp.sum(acc_ref[pl.ds(head + first, size), :], axis=1, keepdims=True) * scale
         at = iota((size, LANES), 0) + first
-        for j in range(slot.shape[0]):
+        for j in range(place.shape[0]):
             mine = jnp.where(at == place[j : j + 1, :], sums, 0.0)
             out_ref[j : j + 1, :] = ref[j : j + 1, :] + jnp.sum(mine, axis=0, keepdims=True)
 
@@ -263,7 +278,7 @@
         + [pl.BlockSpec(memory_space=pl.ANY) if last else vmem] + [vmem] * len(pairs),
         out_specs=[vmem] * len(outs),
         out_shape=outs,
-        scratch_shapes=[pltpu.VMEM((rows + 2 * SLOTS, width), BF16),
+        scratch_shapes=[pltpu.VMEM((rows + WINDOW, width), BF16),
                         pltpu.VMEM((rows, LANES), F32),
                         *copies],
         compiler_params=pltpu.CompilerParams(vmem_limit_bytes=(40 if last else 24) * 2**20),

time: 63.5 us -> 61.8 us (0.973)
  Pallas kernels: 32.4 us -> 30.9 us
    pallas_call x2, Pallas kernels: 26.2 us -> 25 us  [gain(): pl.pallas_call(body, in_specs=[pl.BlockSpec(memory_space=pltpu.SMEM)] * 2...]
  transfers between devices with their start and end apart: 9 -> 9, of which waited for: 8 -> 8; matrix products, arithmetic and copies ran while one was open for 1% -> 1% of each run, Pallas kernels for 17% -> 16%
where the time goes in v3:
time: 61.8 us; the launch traced here: 61.6 us
  Pallas kernels  30.9 us (50%)
  starting transfers between devices  11.5 us (19%)
  waiting for transfers between devices  8.37 us (14%)
  blocking collectives  8.32 us (13%)
  between operations  0.73 us (1%)
  loops' own time  0.65 us (1%)
  local copies, waits for them, and re-layouts  0.62 us (1%)
    pallas_call x2, Pallas kernels, gain(): pl.pallas_call(body, in_specs=[pl.BlockSpec(memory_space=pltpu.SMEM)] * 2...  25 us
    ppermute x9, starting transfers between devices, moved(): return lax.ppermute(array, 'ground', pairs)  11.5 us
    ppermute x9, waiting for transfers between devices, moved(): return lax.ppermute(array, 'ground', pairs)  8.37 us
    all_to_all x1, blocking collectives, body(): arrived = lax.all_to_all(blocks, 'ground', 0, 0, tiled=True)  8.32 us
    pallas_call x1, Pallas kernels, pick(): pl.pallas_call(pick_kernel, in_specs=[pl.BlockSpec(memory_space=pltpu.SME...  5.9 us
  transfers between devices with their start and end apart: 9, of which 8 were waited for; matrix products, arithmetic and copies ran while one was open for 1% of the time, Pallas kernels for 16%

profile of v3, /device:TPU:1, one launch (start us, length us, event | category | flops | bytes accessed | tf_op | source)
XLA Modules:
  0.0 61.6 jit_solution(8808119128179342121)
XLA Ops:
  0.7 5.9 %pick.2 = (bf16[104,1024]{1,0:T(8,128)(2,1)S(1)}, s32[8,128]{1,0:T(8,128)S(1)}, s32[8,128]{1,0:T(8,128)S(1)}) custom-call(s32[1]{0:T(128)} %constant.4.clone.1.turn_ref, s32[8,128]{1,0:T(8,128)} %bitcast.9, s32[1,64]{1,0:T(1,128)} %bitcast.13, bf16[8192,1024]{1,0:T(8,128)(2,1)} %refs_7_.3), custom_call_target="tpu_custom_call" | custom-call | tf_op jit(solution)/shard_map/pick/pallas_call | solution.py:109
  6.6 2.7 %collective-permute-start.11 = (bf16[104,1024]{1,0:T(8,128)(2,1)S(1)}, bf16[104,1024]{1,0:T(8,128)(2,1)S(1)}, u32[]{:S(2)}, u32[]{:S(2)}) collective-permute-start(bf16[104,1024]{1,0:T(8,128)(2,1)S(1)} %get-tuple-element.66.own_ref), channel_id=1, source_target_pairs={{0,2},{1,3},{2,0},{3,1},{4,6},{5,7},{6,4},{7,5},{8,10},{9,11},{10,... | collective-permute-start | bytes 638984 | tf_op jit(solution)/shard_map/ppermute | solution.py:298
  9.3 0.6 collective-permute-start.10
  9.9 2.1 %collective-permute-start.9 = (bf16[104,1024]{1,0:T(8,128)(2,1)S(1)}, bf16[104,1024]{1,0:T(8,128)(2,1)S(1)}, u32[]{:S(2)}, u32[]{:S(2)}) collective-permute-start(bf16[104,1024]{1,0:T(8,128)(2,1)S(1)} %get-tuple-element.66.own_ref), channel_id=1, source_target_pairs={{0,4},{1,13},{2,6},{3,15},{4,8},{5,1},{6,10},{7,3},{8,12},{9,5},{1... | collective-permute-start | bytes 638984 | tf_op jit(solution)/shard_map/ppermute | solution.py:298
  11.9 2.3 %collective-permute-done.11.flip_ref = bf16[104,1024]{1,0:T(8,128)(2,1)S(1)} collective-permute-done((bf16[104,1024]{1,0:T(8,128)(2,1)S(1)}, bf16[104,1024]{1,0:T(8,128)(2,1)S(1)}, u32[]{:S(2)}, u32[]{:S(2)}) %collective-permute-start.11) | collective-permute-done | bytes 213024 | tf_op jit(solution)/shard_map/ppermute | solution.py:298
  14.3 0.9 %collective-permute-done.10.behind_ref = bf16[104,1024]{1,0:T(8,128)(2,1)S(1)} collective-permute-done((bf16[104,1024]{1,0:T(8,128)(2,1)S(1)}, bf16[104,1024]{1,0:T(8,128)(2,1)S(1)}, u32[]{:S(2)}, u32[]{:S(2)}) %collective-permute-start.10) | collective-permute-done | bytes 213024 | tf_op jit(solution)/shard_map/ppermute | solution.py:298
  15.2 1.3 %collective-permute-done.9.ahead_ref = bf16[104,1024]{1,0:T(8,128)(2,1)S(1)} collective-permute-done((bf16[104,1024]{1,0:T(8,128)(2,1)S(1)}, bf16[104,1024]{1,0:T(8,128)(2,1)S(1)}, u32[]{:S(2)}, u32[]{:S(2)}) %collective-permute-start.9) | collective-permute-done | bytes 213024 | tf_op jit(solution)/shard_map/ppermute | solution.py:298
  16.5 3.4 %collective-permute-start.12 = (bf16[208,1024]{1,0:T(8,128)(2,1)S(1)}, bf16[208,1024]{1,0:T(8,128)(2,1)S(1)}, u32[]{:S(2)}, u32[]{:S(2)}) collective-permute-start(bf16[208,1024]{1,0:T(8,128)(2,1)S(1)} %get-tuple-element.67.refs_8_), channel_id=1, source_target_pairs={{0,1},{1,0},{2,3},{3,2},{4,5},{5,4},{6,7},{7,6},{8,9},{9,8},{10,11... | collective-permute-start | bytes 1277960 | tf_op jit(solution)/shard_map/ppermute | solution.py:298
  19.9 0.1 collective-permute-start.13
  20.0 0.8 %collective-permute-start.15 = (bf16[208,1024]{1,0:T(8,128)(2,1)S(1)}, bf16[208,1024]{1,0:T(8,128)(2,1)S(1)}, u32[]{:S(2)}, u32[]{:S(2)}) collective-permute-start(bf16[208,1024]{1,0:T(8,128)(2,1)S(1)} %get-tuple-element.67.refs_8_), channel_id=1, source_target_pairs={{0,6},{1,15},{2,4},{3,13},{4,10},{5,3},{6,8},{7,1},{8,14},{9,7},{1... | collective-permute-start | bytes 1277960 | tf_op jit(solution)/shard_map/ppermute | solution.py:298
  20.9 0.6 collective-permute-start.14
  21.5 0.5 collective-permute-done.13.refs_11_
  22.0 10.1 %gain.1 = (f32[8,128]{1,0:T(8,128)S(1)}, f32[64,128]{1,0:T(8,128)}) custom-call(s32[2]{0:T(128)S(1)} %broadcast_1_refs_0_.2.refs_0_, s32[8,128]{1,0:T(8,128)S(1)} %get-tuple-element.64.refs_1_, s32[8,128]{1,0:T(8,128)S(1)} %bitcast.10, s32[8,128]{1,0:T(8,128)S(1)} %get-tuple-element.65.refs_3_, f32[8,128]{1,0:T(8,128)S(1)} %broadcast_in_dim.3.refs_4_, ...), custom_call_target="tpu_custom_call" | custom-call | flops 7516192768 | bytes 16777216 | tf_op jit(solution)/shard_map/gain/pallas_call | solution.py:275
  32.0 0.5 collective-permute-done.15.refs_13_
  32.5 1.4 %collective-permute-done.14.refs_12_ = bf16[208,1024]{1,0:T(8,128)(2,1)S(1)} collective-permute-done((bf16[208,1024]{1,0:T(8,128)(2,1)S(1)}, bf16[208,1024]{1,0:T(8,128)(2,1)S(1)}, u32[]{:S(2)}, u32[]{:S(2)}) %collective-permute-start.14) | collective-permute-done | bytes 426016 | tf_op jit(solution)/shard_map/ppermute | solution.py:298
  33.9 1.2 %collective-permute-start.16 = (bf16[208,1024]{1,0:T(8,128)(2,1)S(1)}, bf16[208,1024]{1,0:T(8,128)(2,1)S(1)}, u32[]{:S(2)}, u32[]{:S(2)}) collective-permute-start(bf16[208,1024]{1,0:T(8,128)(2,1)S(1)} %collective-permute-done.14.refs_12_), channel_id=1, source_target_pairs={{0,1},{1,0},{2,3},{3,2},{4,5},{5,4},{6,7},{7,6},{8,9},{9,8},{10,11... | collective-permute-start | bytes 1277960 | tf_op jit(solution)/shard_map/ppermute | solution.py:298
  35.1 0.5 slice.3
  35.6 0.9 %collective-permute-done.16.refs_14_ = bf16[208,1024]{1,0:T(8,128)(2,1)S(1)} collective-permute-done((bf16[208,1024]{1,0:T(8,128)(2,1)S(1)}, bf16[208,1024]{1,0:T(8,128)(2,1)S(1)}, u32[]{:S(2)}, u32[]{:S(2)}) %collective-permute-start.16) | collective-permute-done | bytes 426016 | tf_op jit(solution)/shard_map/ppermute | solution.py:298
  36.5 0.6 collective-permute-done.17.refs_15_
  37.1 14.9 %gain_last.2 = (f32[8,128]{1,0:T(8,128)S(1)}, f32[64,128]{1,0:T(8,128)S(1)}) custom-call(s32[2]{0:T(128)S(1)} %iota_multiply_fusion.refs_0_, s32[8,128]{1,0:T(8,128)S(1)} %get-tuple-element.64.refs_1_, s32[8,128]{1,0:T(8,128)S(1)} %bitcast.11, s32[8,128]{1,0:T(8,128)S(1)} %get-tuple-element.65.refs_3_, f32[8,128]{1,0:T(8,128)S(1)} %get-tuple-element.70.refs_4_, ...), custom_call_target="tpu_custom_call" | custom-call | flops 10737418240 | bytes 16777216 | tf_op jit(solution)/shard_map/gain_last/pallas_call | solution.py:275
  52.0 0.7 %while.12 = (s32[]{:T(128)}, f32[8,128]{1,0:T(8,128)S(1)}, f32[64,128]{1,0:T(8,128)S(1)}, s32[]{:T(128)}, s32[8,128]{1,0:T(8,128)S(1)}, /*index=5*/s32[1,64]{1,0...) while((s32[]{:T(128)}, f32[8,128]{1,0:T(8,128)S(1)}, ...), condition=%wide.region_1.0_spmd, body=%wide.region_0.0_spmd.sunk | while | flops 10737418240 | bytes 29630948 | solution.py:379
  52.7 0.1 div.10
  52.8 8.3 %all_to_all.6 = f32[16,1,64]{2,1,0:T(1,128)S(1)} all-to-all(f32[16,1,64]{2,1,0:T(1,128)S(1)} %div.10), channel_id=1, replica_groups=mesh['cand'=8,'ground'=16] {'ground'}, dimensions={0} | all-to-all | bytes 8192 | tf_op jit(solution)/shard_map/all_to_all | solution.py:381
  61.1 0.5 reduce_sum.9
  (17 shorter events, 0.1 us)
Async XLA Ops:
  0.6 21.3 %copy-start = (bf16[8192,1024]{1,0:T(8,128)(2,1)S(1)}, bf16[8192,1024]{1,0:T(8,128)(2,1)}, u32[]{:S(2)}) copy-start(bf16[8192,1024]{1,0:T(8,128)(2,1)} %refs_7_.3) | copy-start | bytes 50331652
  0.6 21.3 %copy-start.2 = (s32[1024]{0:T(1024)S(1)}, s32[1024]{0:T(1024)}, u32[]{:S(2)}) copy-start(s32[1024]{0:T(1024)} %param.8) | copy-start | bytes 12292
  0.7 21.3 %copy-start.4 = (f32[8192]{0:T(1024)S(1)}, f32[8192]{0:T(1024)}, u32[]{:S(2)}) copy-start(f32[8192]{0:T(1024)} %param.7) | copy-start | bytes 98308
  6.6 7.7 %collective-permute-start.11 = (bf16[104,1024]{1,0:T(8,128)(2,1)S(1)}, bf16[104,1024]{1,0:T(8,128)(2,1)S(1)}, u32[]{:S(2)}, u32[]{:S(2)}) collective-permute-start(bf16[104,1024]{1,0:T(8,128)(2,1)S(1)} %get-tuple-element.66.own_ref), channel_id=1, source_target_pairs={{0,2},{1,3},{2,0},{3,1},{4,6},{5,7},{6,4},{7,5},{8,10},{9,11},{10,... | collective-permute-start | bytes 638984 | tf_op jit(solution)/shard_map/ppermute | solution.py:298
  9.3 5.9 %collective-permute-start.10 = (bf16[104,1024]{1,0:T(8,128)(2,1)S(1)}, bf16[104,1024]{1,0:T(8,128)(2,1)S(1)}, u32[]{:S(2)}, u32[]{:S(2)}) collective-permute-start(bf16[104,1024]{1,0:T(8,128)(2,1)S(1)} %get-tuple-element.66.own_ref), channel_id=1, source_target_pairs={{0,12},{1,5},{2,14},{3,7},{4,0},{5,9},{6,2},{7,11},{8,4},{9,13},{1... | collective-permute-start | bytes 638984 | tf_op jit(solution)/shard_map/ppermute | solution.py:298
  9.9 6.6 %collective-permute-start.9 = (bf16[104,1024]{1,0:T(8,128)(2,1)S(1)}, bf16[104,1024]{1,0:T(8,128)(2,1)S(1)}, u32[]{:S(2)}, u32[]{:S(2)}) collective-permute-start(bf16[104,1024]{1,0:T(8,128)(2,1)S(1)} %get-tuple-element.66.own_ref), channel_id=1, source_target_pairs={{0,4},{1,13},{2,6},{3,15},{4,8},{5,1},{6,10},{7,3},{8,12},{9,5},{1... | collective-permute-start | bytes 638984 | tf_op jit(solution)/shard_map/ppermute | solution.py:298
  16.5 4.9 %collective-permute-start.12 = (bf16[208,1024]{1,0:T(8,128)(2,1)S(1)}, bf16[208,1024]{1,0:T(8,128)(2,1)S(1)}, u32[]{:S(2)}, u32[]{:S(2)}) collective-permute-start(bf16[208,1024]{1,0:T(8,128)(2,1)S(1)} %get-tuple-element.67.refs_8_), channel_id=1, source_target_pairs={{0,1},{1,0},{2,3},{3,2},{4,5},{5,4},{6,7},{7,6},{8,9},{9,8},{10,11... | collective-permute-start | bytes 1277960 | tf_op jit(solution)/shard_map/ppermute | solution.py:298
  19.9 2.0 %collective-permute-start.13 = (bf16[208,1024]{1,0:T(8,128)(2,1)S(1)}, bf16[208,1024]{1,0:T(8,128)(2,1)S(1)}, u32[]{:S(2)}, u32[]{:S(2)}) collective-permute-start(bf16[208,1024]{1,0:T(8,128)(2,1)S(1)} %get-tuple-element.68.refs_9_), channel_id=1, source_target_pairs={{0,1},{1,0},{2,3},{3,2},{4,5},{5,4},{6,7},{7,6},{8,9},{9,8},{10,11... | collective-permute-start | bytes 1277960 | tf_op jit(solution)/shard_map/ppermute | solution.py:298
  20.0 12.5 %collective-permute-start.15 = (bf16[208,1024]{1,0:T(8,128)(2,1)S(1)}, bf16[208,1024]{1,0:T(8,128)(2,1)S(1)}, u32[]{:S(2)}, u32[]{:S(2)}) collective-permute-start(bf16[208,1024]{1,0:T(8,128)(2,1)S(1)} %get-tuple-element.67.refs_8_), channel_id=1, source_target_pairs={{0,6},{1,15},{2,4},{3,13},{4,10},{5,3},{6,8},{7,1},{8,14},{9,7},{1... | collective-permute-start | bytes 1277960 | tf_op jit(solution)/shard_map/ppermute | solution.py:298
  20.9 13.0 %collective-permute-start.14 = (bf16[208,1024]{1,0:T(8,128)(2,1)S(1)}, bf16[208,1024]{1,0:T(8,128)(2,1)S(1)}, u32[]{:S(2)}, u32[]{:S(2)}) collective-permute-start(bf16[208,1024]{1,0:T(8,128)(2,1)S(1)} %get-tuple-element.68.refs_9_), channel_id=1, source_target_pairs={{0,12},{1,5},{2,14},{3,7},{4,0},{5,9},{6,2},{7,11},{8,4},{9,13},{1... | collective-permute-start | bytes 1277960 | tf_op jit(solution)/shard_map/ppermute | solution.py:298
  33.9 2.6 %collective-permute-start.16 = (bf16[208,1024]{1,0:T(8,128)(2,1)S(1)}, bf16[208,1024]{1,0:T(8,128)(2,1)S(1)}, u32[]{:S(2)}, u32[]{:S(2)}) collective-permute-start(bf16[208,1024]{1,0:T(8,128)(2,1)S(1)} %collective-permute-done.14.refs_12_), channel_id=1, source_target_pairs={{0,1},{1,0},{2,3},{3,2},{4,5},{5,4},{6,7},{7,6},{8,9},{9,8},{10,11... | collective-permute-start | bytes 1277960 | tf_op jit(solution)/shard_map/ppermute | solution.py:298
  35.1 2.0 %collective-permute-start.17 = (bf16[208,1024]{1,0:T(8,128)(2,1)S(1)}, bf16[208,1024]{1,0:T(8,128)(2,1)S(1)}, u32[]{:S(2)}, u32[]{:S(2)}) collective-permute-start(bf16[208,1024]{1,0:T(8,128)(2,1)S(1)} %collective-permute-done.15.refs_13_), channel_id=1, source_target_pairs={{0,1},{1,0},{2,3},{3,2},{4,5},{5,4},{6,7},{7,6},{8,9},{9,8},{10,11... | collective-permute-start | bytes 1277960 | tf_op jit(solution)/shard_map/ppermute | solution.py:298
  35.6 16.4 %copy-start.3 = (s32[64]{0:T(128)S(1)}, s32[64]{0:T(128)}, u32[]{:S(2)}) copy-start(s32[64]{0:T(128)} %param.9) | copy-start | bytes 772
  52.7 9.0 %copy-start.1 = (f32[64,128]{1,0:T(8,128)}, f32[64,128]{1,0:T(8,128)S(1)}, u32[]{:S(2)}) copy-start(f32[64,128]{1,0:T(8,128)S(1)} %get-tuple-element.76) | copy-start | bytes 98308
